TPU v7x, 256 devices: a whole 4x4x8 slice. The times are simulated.
256 devices in a mesh: wide: 32 (over z, x), mom: 8 (over y, core).
Axes of the slice: x: 4, y: 4, z: 8, core: 2. Of those that a mesh axis runs over, the one named last changes fastest.
Arguments:
- green_blocks: bfloat16 [64, 8, 1024, 256], P('wide', 'mom'), may hold values from -6 to 6
- neighbours: int32 [1024, 4], P(('wide', 'mom')), may hold values from 0 to 1023, as said below
- counts: int32 [1024], P(('wide', 'mom')), may hold values from 1 to 4, as said below
- couplings: float32 [1024, 4, 8, 4], P(('wide', 'mom')), may hold values from 0.01 to 0.1
- grad_h: bfloat16 [1024, 4, 16, 16], P(('wide', 'mom')), may hold values from -1.5 to 1.5
- momentum_table: int32 [8, 8], replicated, may hold values from 0 to 7, each once within a row
Outputs:
- self_energy: bfloat16 [64, 8, 1024, 256], P('wide', 'mom')
Inputs may be any that keep to these rules, and one draw needn't show every extreme that they name: `neighbours`: the first counts[a] slots of row a hold distinct atoms other than a, each within 2 positions of a; the remaining slots hold a itself. `counts`: some atom uses all 4 slots. `momentum_table`: each row is a permutation of the momentum points.
All inputs are finite; a program needn't handle non-finite values.
Results may differ from a plain program's by a relative error of at most 0.0064.
Values may be sent and summed in bfloat16 or wider, within the bound.
No kernel may reach another device: no remote copies, remote signals or barrier semaphores. Data moves between devices by JAX's collectives and lax.ppermute only.
A program may use at most 64 MiB of HBM per device.

v0:
```python
import jax
import jax.numpy as jnp
from jax import lax
from jax.sharding import PartitionSpec as P

REACH = 2
NW = 2
ESTEP = 3


def cut_along(shard, dim, count):
    before, after = (shard.shape[:dim], shard.shape[dim + 1 :])
    return jnp.moveaxis(shard.reshape(*before, count, -1, *after), dim, 0)


def laid_out(blocks, dim):
    blocks = jnp.moveaxis(blocks, 0, dim)
    lengths = blocks.shape
    return blocks.reshape(*lengths[:dim], lengths[dim] * lengths[dim + 1], *lengths[dim + 2 :])


def exchange_both(shard, axis, axes, splits, concats):
    sizes = [lax.axis_size(a) for a in axes]
    blocks = cut_along(shard, splits[0], sizes[0])
    blocks = jnp.moveaxis(cut_along(blocks, splits[1] + 1, sizes[1]), 0, 1)
    inside = blocks.shape[2:]
    blocks = blocks.reshape(-1, *inside)
    blocks = lax.all_to_all(blocks, axis, split_axis=0, concat_axis=0, tiled=True)
    blocks = laid_out(blocks.reshape(*sizes, *inside), concats[0] + 1)
    return laid_out(blocks, concats[1])


def padded_2(shard, sides, width):
    edges = {}
    for axis, dim in sides:
        count, length = (lax.axis_size(axis), shard.shape[dim])
        up = [(i, (i + 1) % count) for i in range(count - 1)]
        last = lax.slice_in_dim(shard, length - width, length, axis=dim)
        first = lax.slice_in_dim(shard, 0, width, axis=dim)
        edges[dim] = (
            lax.ppermute(last, axis, up),
            lax.ppermute(first, axis, [(b, a) for a, b in up]),
        )
    done = []
    for _, dim in sides:
        low, high = edges[dim]
        around = [(width, width) if d in done else (0, 0) for d in range(shard.ndim)]
        shard = jnp.concatenate([jnp.pad(low, around), shard, jnp.pad(high, around)], axis=dim)
        done.append(dim)
    return shard


def shift_list(mode_count, spacing):
    upward = [(mode_idx + 1) * spacing for mode_idx in range(mode_count)]
    downward = [-(mode_idx + 1) * spacing for mode_idx in range(mode_count)]
    return upward + downward


def coupling_weights(couplings, counts, momentum_table):
    momenta = momentum_table.shape[0]
    routing = (
        momentum_table[:, :, None] == jnp.arange(momenta, dtype=jnp.int32)[None, None, :]
    ).astype(jnp.float32)
    slots_used = (
        jnp.arange(couplings.shape[1], dtype=jnp.int32)[None, :] < counts[:, None]
    ).astype(jnp.float32)
    masked = couplings * slots_used[:, :, None, None]
    combined = jnp.einsum("abqs,kql->abkls", masked, routing, precision=lax.Precision.HIGHEST)
    return combined.astype(jnp.bfloat16)


def kron_blocks(grad_h):
    matrix = grad_h.astype(jnp.float32)
    orbitals = matrix.shape[-1]
    product = matrix[..., :, None, :, None] * matrix[..., None, :, None, :]
    return product.reshape(matrix.shape[:-2] + (orbitals * orbitals, orbitals * orbitals)).astype(
        jnp.bfloat16
    )


def body(green_blocks, neighbours, counts, couplings, grad_h, momentum_table):
    atom_count = neighbours.shape[0]
    atom_major = exchange_both(green_blocks, ("wide", "mom"), ("wide", "mom"), (2, 2), (0, 1))
    extended = padded_2(atom_major, ((("wide", "mom"), 2),), REACH)
    first_atom = lax.axis_index(("wide", "mom")) * atom_count - REACH
    positions = neighbours - first_atom
    weights = coupling_weights(couplings, counts, momentum_table)
    kron_mats = kron_blocks(grad_h)
    shifts = shift_list(NW, ESTEP)
    margin = NW * ESTEP
    energy_total = extended.shape[0]
    running = jnp.zeros(
        (extended.shape[0], extended.shape[1], atom_count, extended.shape[3]), jnp.float32
    )
    slot_count = neighbours.shape[1]
    for slot_id in range(slot_count):
        column = lax.dynamic_index_in_dim(positions, slot_id, axis=1, keepdims=False)
        near_blocks = jnp.take(extended, column, axis=2)
        padded = jnp.pad(near_blocks, ((margin, margin), (0, 0), (0, 0), (0, 0)))
        stacked = jnp.stack(
            [padded[margin - amount : margin - amount + energy_total] for amount in shifts], axis=0
        )
        slot_weights = lax.dynamic_index_in_dim(weights, slot_id, axis=1, keepdims=False)
        slot_kron = lax.dynamic_index_in_dim(kron_mats, slot_id, axis=1, keepdims=False)
        blended = jnp.einsum(
            "akls,selax->ekax", slot_weights, stacked, preferred_element_type=jnp.float32
        )
        blended = blended.astype(jnp.bfloat16)
        running = running + jnp.einsum(
            "ekax,axy->ekay", blended, slot_kron, preferred_element_type=jnp.float32
        )
    rounded = running.astype(jnp.bfloat16)
    regrouped = rounded.reshape(
        (rounded.shape[0], rounded.shape[1], 1, 1, atom_count, rounded.shape[3])
    )
    returned = exchange_both(regrouped, ("wide", "mom"), ("wide", "mom"), (0, 1), (2, 3))
    return returned.reshape((returned.shape[0], returned.shape[1], -1, returned.shape[-1]))


def solution(mesh):
    in_specs = (
        P("wide", "mom", None, None),
        P(("wide", "mom"), None),
        P(("wide", "mom")),
        P(("wide", "mom"), None, None, None),
        P(("wide", "mom"), None, None, None),
        P(),
    )
    out_specs = P("wide", "mom", None, None)
    return jax.shard_map(body, mesh=mesh, in_specs=in_specs, out_specs=out_specs, check_vma=False)
```

profile of v0, /device:TPU:1, one launch (start us, length us, event | category | flops | bytes accessed | tf_op | source)
XLA Modules:
  0.0 141.0 jit_solution(6165414811900310632)
XLA Ops:
  0.0 1.8 %copy.60 = bf16[32,2,1,32,256]{4,0,3,1,2:T(8,128)(2,1)S(1)} copy(bf16[32,2,1,32,256]{4,3,0,1,2:T(8,128)(2,1)} %bitcast.176) | data formatting | bytes 2097152 | tf_op jit(solution)/shard_map/transpose | solution.py:13
  1.8 0.6 copy.164
  2.5 1.8 %copy.62 = bf16[256,2,1,4,256]{4,3,1,2,0:T(4,128)(2,1)} copy(bf16[256,2,1,4,256]{4,0,3,1,2:T(8,128)(2,1)S(1)} %bitcast.171) | data formatting | bytes 2097152 | tf_op jit(solution)/shard_map/reshape | solution.py:27
  4.2 15.6 %all-to-all-start = ((bf16[256,2,1,4,256]{4,3,1,2,0:T(4,128)(2,1)}), bf16[256,2,1,4,256]{4,3,1,2,0:T(4,128)(2,1)S(1)}, u32[]{:S(2)}, u32[]{:S(2)}) async-start(bf16[256,2,1,4,256]{4,3,1,2,0:T(4,128)(2,1)} %copy.62), calls=%async_computation | async-start | bytes 2097152 | tf_op jit(solution)/shard_map/all_to_all | solution.py:28
  19.9 6.2 %multiply_convert_fusion = bf16[4,4,16,16,16,16]{5,4,3,2,0,1:T(8,128)(2,1)} fusion(bf16[4,4,16,16]{3,2,1,0:T(8,128)(2,1)S(1)} %copy-done.4), kind=kLoop, calls=%fused_computation.4 | loop fusion | flops 2097152 | bytes 2105344 | tf_op jit(solution)/shard_map/convert_element_type | solution.py:76
  26.1 20.6 %convert_element_type.60 = bf16[4,4,256,256]{3,2,0,1:T(8,128)(2,1)} reshape(bf16[4,4,16,16,16,16]{5,4,3,2,0,1:T(8,128)(2,1)} %multiply_convert_fusion) | data formatting | bytes 4194304 | tf_op jit(solution)/shard_map/convert_element_type | solution.py:76
  47.1 3.2 %all-to-all-done = bf16[256,2,1,4,256]{4,3,1,2,0:T(4,128)(2,1)S(1)} async-done(((bf16[256,2,1,4,256]{4,3,1,2,0:T(4,128)(2,1)}), bf16[256,2,1,4,256]{4,3,1,2,0:T(4,128)(2,1)S(1)}, u32[]{:S(2)}, u32[]{:S(2)}) %all-to-all-start) | async-done | bytes 1048608 | tf_op jit(solution)/shard_map/all_to_all | solution.py:28
  50.8 3.4 %collective-permute-start.1 = (bf16[64,8,2,256]{3,1,2,0:T(8,128)(2,1)S(1)}, bf16[64,8,2,256]{3,1,2,0:T(8,128)(2,1)S(1)}, u32[]{:S(2)}, u32[]{:S(2)}) collective-permute-start(bf16[64,8,2,256]{3,1,2,0:T(8,128)(2,1)S(1)} %get-tuple-element.27), channel_id=1, source_target_pairs={{1,0},{2,1},{3,2},{4,3},{5,4},{6,5},{7,6},{8,7},{9,8},{10,9},{11,1... | collective-permute-start | bytes 1572872 | tf_op jit(solution)/shard_map/ppermute | solution.py:42
  54.2 2.2 %collective-permute-start = (bf16[64,8,2,256]{3,1,2,0:T(8,128)(2,1)S(1)}, bf16[64,8,2,256]{3,1,2,0:T(8,128)(2,1)S(1)}, u32[]{:S(2)}, u32[]{:S(2)}) collective-permute-start(bf16[64,8,2,256]{3,1,2,0:T(8,128)(2,1)S(1)} %get-tuple-element.26), channel_id=1, source_target_pairs={{0,1},{1,2},{2,3},{3,4},{4,5},{5,6},{6,7},{7,8},{8,9},{9,10},{10,1... | collective-permute-start | bytes 1572872 | tf_op jit(solution)/shard_map/ppermute | solution.py:41
  56.9 4.4 %collective-permute-done.1 = bf16[64,8,2,256]{3,1,2,0:T(8,128)(2,1)S(1)} collective-permute-done((bf16[64,8,2,256]{3,1,2,0:T(8,128)(2,1)S(1)}, bf16[64,8,2,256]{3,1,2,0:T(8,128)(2,1)S(1)}, u32[]{:S(2)}, u32[]{:S(2)}) %collective-permute-start.1) | collective-permute-done | bytes 524320 | tf_op jit(solution)/shard_map/ppermute | solution.py:42
  61.3 1.2 collective-permute-done
  62.7 0.7 gather_fusion.2
  64.1 1.5 %fusion.2 = bf16[4,64,256,8,1]{2,3,1,0,4:T(8,128)(2,1)S(1)} fusion(bf16[4,8,8,4,1]{2,3,0,1,4:T(4,128)(2,1)S(1)} %get-tuple-element.29, bf16[1,64,8,4,256]{4,2,3,1,0:T(8,128)(2,1)S(1)} %get-tuple-element.25, bf16[1,64,8,4,256]{4,2,3,1,0:T(8,128)(2,1)S(1)} %get-tuple-element.24, bf16[1,64,8,4,256]{4,2,3,1,0:T(8,128)(2,1)S(1)} %get-tuple-element.23, ...), kind=kOutput, calls=%fused_computation.11 | convolution fusion | flops 39845888 | bytes 5244928 | tf_op jit(solution)/shard_map/akls,selax->ekax/dot_general | solution.py:105
  65.7 1.7 %gather_fusion = bf16[4,64,8,256]{3,2,1,0:T(8,128)(2,1)} fusion(bf16[64,8,8,256]{3,1,2,0:T(8,128)(2,1)S(1)} %pad_maximum_fusion.4, s32[1024]{0:T(1024)S(1)} %pad_clamp_fusion.3), kind=kCustom, calls=%fused_computation.clone | custom fusion | bytes 2097168 | tf_op jit(solution)/shard_map/jit(_take)/gather | solution.py:98
  67.4 1.4 fusion.40
  69.3 1.3 fusion.6
  70.8 1.4 %copy-done = bf16[4,4,256,256]{3,2,0,1:T(8,128)(2,1)S(1)} copy-done((bf16[4,4,256,256]{3,2,0,1:T(8,128)(2,1)S(1)}, bf16[4,4,256,256]{3,2,0,1:T(8,128)(2,1)}, u32[]{:S(2)}) %copy-start) | copy-done | bytes 2097176
  72.2 2.6 %fusion.32 = f32[4,256,64,8]{1,2,3,0:T(8,128)} fusion(bf16[64,8,4,256]{3,1,2,0:T(8,128)(2,1)S(1)} %bitcast.167, bf16[4,4,256,256]{3,2,0,1:T(8,128)(2,1)S(1)} %copy-done), kind=kOutput, calls=%fused_computation.66 | convolution fusion | flops 268435456 | bytes 3670016 | tf_op jit(solution)/shard_map/ekax,axy->ekay/dot_general | solution.py:109
  74.8 2.6 %fusion.38 = f32[4,256,64,8]{1,2,3,0:T(8,128)} fusion(bf16[64,8,4,256]{3,1,2,0:T(8,128)(2,1)S(1)} %bitcast.169, bf16[4,4,256,256]{3,2,0,1:T(8,128)(2,1)S(1)} %copy-done), kind=kOutput, calls=%fused_computation.74 | convolution fusion | flops 268435456 | bytes 3670016 | tf_op jit(solution)/shard_map/ekax,axy->ekay/dot_general | solution.py:109
  77.4 0.7 gather_fusion.1
  78.8 1.3 fusion.4
  80.2 3.6 %fusion.35 = f32[4,256,64,8]{1,2,3,0:T(8,128)} fusion(bf16[64,8,4,256]{3,1,2,0:T(8,128)(2,1)S(1)} %bitcast.170, bf16[4,4,256,256]{3,2,0,1:T(8,128)(2,1)} %convert_element_type.60), kind=kOutput, calls=%fused_computation.70 | convolution fusion | flops 268435456 | bytes 3670016 | tf_op jit(solution)/shard_map/ekax,axy->ekay/dot_general | solution.py:109
  83.9 0.7 gather_fusion.3
  85.3 1.3 fusion
  86.8 0.6 copy-done.3
  87.5 0.9 copy-done.1
  88.4 2.6 %fusion.8 = bf16[64,8,4,256]{3,0,1,2:T(8,128)(2,1)S(1)} fusion(f32[4,256,64,8]{1,2,3,0:T(8,128)S(1)} %copy-done.1, f32[4,256,64,8]{1,2,3,0:T(8,128)S(1)} %copy-done.2, f32[4,256,64,8]{1,2,3,0:T(8,128)S(1)} %copy-done.3, bf16[64,8,4,256]{3,1,2,0:T(8,128)(2,1)S(1)} %bitcast.168, bf16[4,4,256,256]{3,2,0,1:T(8,128)(2,1)} %convert_element_type.60), kind=kOutput, calls=%fused_computation.23 | convolution fusion | flops 270532608 | bytes 8912896 | tf_op jit(solution)/shard_map/ekax,axy->ekay/dot_general | solution.py:109
  91.5 0.6 copy.162
  92.1 0.8 copy.78
  92.9 46.4 %all_to_all.10 = bf16[256,2,1,1,1,4,256]{6,5,1,4,3,2,0:T(4,128)(2,1)S(1)} all-to-all(bf16[256,2,1,1,1,4,256]{6,5,1,4,3,2,0:T(4,128)(2,1)S(1)} %copy.78), channel_id=1, replica_groups=mesh['wide'=32,'mom'=8] {'wide','mom'}, dimensions={0} | all-to-all | bytes 2097152 | tf_op jit(solution)/shard_map/all_to_all | solution.py:28
  139.3 0.6 copy.79
  139.9 1.1 reshape_reshape.3
  (44 shorter events, 5.1 us)
Async XLA Ops:
  2.4 17.5 %copy-start.4 = (bf16[4,4,16,16]{3,2,1,0:T(8,128)(2,1)S(1)}, bf16[4,4,16,16]{3,2,1,0:T(8,128)(2,1)}, u32[]{:S(2)}) copy-start(bf16[4,4,16,16]{3,2,1,0:T(8,128)(2,1)} %param.12) | copy-start | bytes 24580
  4.2 46.1 %all-to-all-start = ((bf16[256,2,1,4,256]{4,3,1,2,0:T(4,128)(2,1)}), bf16[256,2,1,4,256]{4,3,1,2,0:T(4,128)(2,1)S(1)}, u32[]{:S(2)}, u32[]{:S(2)}) async-start(bf16[256,2,1,4,256]{4,3,1,2,0:T(4,128)(2,1)} %copy.62), calls=%async_computation | async-start | bytes 2097152 | tf_op jit(solution)/shard_map/all_to_all | solution.py:28
  26.1 20.6 %copy-start.7 = (s32[4,4]{1,0:T(4,128)S(1)}, s32[4,4]{1,0:T(4,128)}, u32[]{:S(2)}) copy-start(s32[4,4]{1,0:T(4,128)} %param.9) | copy-start | bytes 196
  26.1 20.9 %copy-start.8 = (s32[4]{0:T(128)S(1)}, s32[4]{0:T(128)}, u32[]{:S(2)}) copy-start(s32[4]{0:T(128)} %param.10) | copy-start | bytes 52
  50.5 5.9 %copy-start.5 = (f32[4,4,8,4]{2,3,1,0:T(4,128)S(1)}, f32[4,4,8,4]{2,3,1,0:T(4,128)}, u32[]{:S(2)}) copy-start(f32[4,4,8,4]{2,3,1,0:T(4,128)} %param.11) | copy-start | bytes 6148
  50.5 5.9 %copy-start.6 = (s32[8,8]{1,0:T(8,128)S(1)}, s32[8,8]{1,0:T(8,128)}, u32[]{:S(2)}) copy-start(s32[8,8]{1,0:T(8,128)} %param.13) | copy-start | bytes 772
  50.8 10.5 %collective-permute-start.1 = (bf16[64,8,2,256]{3,1,2,0:T(8,128)(2,1)S(1)}, bf16[64,8,2,256]{3,1,2,0:T(8,128)(2,1)S(1)}, u32[]{:S(2)}, u32[]{:S(2)}) collective-permute-start(bf16[64,8,2,256]{3,1,2,0:T(8,128)(2,1)S(1)} %get-tuple-element.27), channel_id=1, source_target_pairs={{1,0},{2,1},{3,2},{4,3},{5,4},{6,5},{7,6},{8,7},{9,8},{10,9},{11,1... | collective-permute-start | bytes 1572872 | tf_op jit(solution)/shard_map/ppermute | solution.py:42
  54.2 8.3 %collective-permute-start = (bf16[64,8,2,256]{3,1,2,0:T(8,128)(2,1)S(1)}, bf16[64,8,2,256]{3,1,2,0:T(8,128)(2,1)S(1)}, u32[]{:S(2)}, u32[]{:S(2)}) collective-permute-start(bf16[64,8,2,256]{3,1,2,0:T(8,128)(2,1)S(1)} %get-tuple-element.26), channel_id=1, source_target_pairs={{0,1},{1,2},{2,3},{3,4},{4,5},{5,6},{6,7},{7,8},{8,9},{9,10},{10,1... | collective-permute-start | bytes 1572872 | tf_op jit(solution)/shard_map/ppermute | solution.py:41
  70.6 1.6 %copy-start = (bf16[4,4,256,256]{3,2,0,1:T(8,128)(2,1)S(1)}, bf16[4,4,256,256]{3,2,0,1:T(8,128)(2,1)}, u32[]{:S(2)}) copy-start(bf16[4,4,256,256]{3,2,0,1:T(8,128)(2,1)} %convert_element_type.60) | copy-start | bytes 6291460
  85.2 1.6 %copy-start.2 = (f32[4,256,64,8]{1,2,3,0:T(8,128)S(1)}, f32[4,256,64,8]{1,2,3,0:T(8,128)}, u32[]{:S(2)}) copy-start(f32[4,256,64,8]{1,2,3,0:T(8,128)} %fusion.38) | copy-start | bytes 6291460
  85.2 2.2 %copy-start.3 = (f32[4,256,64,8]{1,2,3,0:T(8,128)S(1)}, f32[4,256,64,8]{1,2,3,0:T(8,128)}, u32[]{:S(2)}) copy-start(f32[4,256,64,8]{1,2,3,0:T(8,128)} %fusion.35) | copy-start | bytes 6291460
  86.6 1.8 %copy-start.1 = (f32[4,256,64,8]{1,2,3,0:T(8,128)S(1)}, f32[4,256,64,8]{1,2,3,0:T(8,128)}, u32[]{:S(2)}) copy-start(f32[4,256,64,8]{1,2,3,0:T(8,128)} %fusion.32) | copy-start | bytes 6291460
where the time goes:
time: 142 us; the launch traced here: 141 us
  blocking collectives  46.4 us (33%)
  local copies, waits for them, and re-layouts  38.4 us (27%)
  starting transfers between devices  21.2 us (15%)
  matrix products  17.3 us (12%)
  waiting for transfers between devices  8.77 us (6%)
  other arithmetic  8.45 us (6%)
    all_to_all x1, blocking collectives, exchange_both(): lax.all_to_all(blocks, axis, split_axis=0, concat_axis=0, tiled=True)  46.4 us
    convert_element_type x1, local copies, waits for them, and re-layouts, kron_blocks(): product.reshape(matrix.shape[:-2] + (orbitals * orbitals, orbitals * orbi...  20.6 us
    all_to_all x1, starting transfers between devices, exchange_both(): lax.all_to_all(blocks, axis, split_axis=0, concat_axis=0, tiled=True)  15.6 us
    dot_general x4, matrix products, body(): jnp.einsum('ekax,axy->ekay', blended, slot_kron, preferred_element_type=j...  11.4 us
    convert_element_type x1, other arithmetic, kron_blocks(): product.reshape(matrix.shape[:-2] + (orbitals * orbitals, orbitals * orbi...  6.22 us
    dot_general x4, matrix products, body(): jnp.einsum('akls,selax->ekax', slot_weights, stacked, preferred_element_t...  5.45 us
    ppermute x1, waiting for transfers between devices, padded_2(): lax.ppermute(first, axis, [(b, a) for a, b in up])  4.41 us
    gather x4, local copies, waits for them, and re-layouts, body(): near_blocks = jnp.take(extended, column, axis=2)  3.72 us
  transfers between devices with their start and end apart: 3, of which 3 were waited for; matrix products, arithmetic and copies ran while one was open for 20% of the time, Pallas kernels for 0%

commit v1 on v0

v1 whole, which is shorter than its diff:
```python
import functools

import jax
import jax.numpy as jnp
from jax import lax
from jax.experimental import pallas as pl
from jax.experimental.pallas import tpu as pltpu
from jax.sharding import Mesh, PartitionSpec as P

REACH = 2
NW = 2
ESTEP = 3

NZ, NX, NM = 8, 4, 8
NO = 16
NB = 4
BLOCK = 32
WIDE_BLOCK = BLOCK + 2 * REACH
COLS = 160
UNROLL = 2


def shifts():
    up = [(i + 1) * ESTEP for i in range(NW)]
    return up + [-d for d in up]


def group_exchange(blocks):
    return lax.all_to_all(blocks, ("x", "m"), split_axis=0, concat_axis=0, tiled=True)


def pack_kernel(green_ref, out_ref):
    for m in range(NM):
        for x in range(NX):
            first = (m * NX + x) * BLOCK
            dest = x * NM + m
            halo = []
            for b in range(2):
                out_ref[dest, b * BLOCK : (b + 1) * BLOCK, :] = green_ref[
                    b, first : first + BLOCK, :
                ]
                left = green_ref[b, max(first - 16, 0) : max(first - 16, 0) + 16, :][16 - REACH :]
                after = min(first + BLOCK, 1024 - 16)
                right = green_ref[b, after : after + 16, :][:REACH]
                halo += [left, right]
            out_ref[dest, 2 * BLOCK :, :] = jnp.concatenate(halo, axis=0)


def packed_blocks(green):
    vmem = pl.BlockSpec(memory_space=pltpu.VMEM)
    return pl.pallas_call(
        pack_kernel,
        out_shape=jax.ShapeDtypeStruct((NX * NM, 2 * WIDE_BLOCK, 256), green.dtype),
        in_specs=[vmem],
        out_specs=vmem,
        cost_estimate=pl.CostEstimate(flops=1 << 22, bytes_accessed=2 << 20, transcendentals=0),
    )(green)


def atom_data(neighbours, counts, couplings, grad_h):
    used = jnp.arange(NB, dtype=jnp.int32)[None, :] < counts[:, None]
    kept = jnp.where(used[:, :, None, None], couplings, 0.0).astype(jnp.bfloat16)
    start = 4 * (
        (lax.axis_index("z") * NX + lax.axis_index("x")) * NM + lax.axis_index("m")
    )
    atoms = start + jnp.arange(4, dtype=jnp.int32)
    offset = (neighbours - atoms[:, None]).astype(jnp.bfloat16)
    rows = jnp.concatenate(
        [
            grad_h.reshape(16, 256),
            kept.reshape(16, 32),
            offset.reshape(16, 1),
            jnp.zeros((16, 95), jnp.bfloat16),
        ],
        axis=1,
    )
    spread = jnp.broadcast_to(rows[None], (NM, 16, 384))
    spread = lax.all_to_all(spread, "m", split_axis=0, concat_axis=0, tiled=True)
    swap = [(z * NM + m, m * NM + z) for z in range(NZ) for m in range(NM)]
    return lax.ppermute(spread, ("z", "m"), swap).reshape(BLOCK * NB, 384)


def banded_weights(kept, momentum_table):
    rows = 2 * NM * 32
    tiled = jnp.tile(kept, (1, 2 * NM))
    lane = jnp.arange(rows, dtype=jnp.int32)
    spread = jnp.where(
        (lane // 32)[None, None, :] == jnp.arange(2 * NM, dtype=jnp.int32)[None, :, None],
        tiled[:, None, :],
        jnp.zeros((), kept.dtype),
    ).reshape(BLOCK * NB * 2 * NM, rows)
    k, b, q, s = lane // 64, lane // 32 % 2, lane // 4 % 8, lane % 4
    shift = jnp.where(s < NW, (s + 1) * ESTEP, (NW - 1 - s) * ESTEP)
    one_hot = (
        jnp.arange(NM, dtype=jnp.int32)[None, :] == k[:, None]
    ).astype(jnp.float32)
    by_k = jnp.dot(one_hot, momentum_table.astype(jnp.float32), precision=lax.Precision.HIGHEST)
    reached = jnp.sum(
        jnp.where(jnp.arange(NM, dtype=jnp.int32)[None, :] == q[:, None], by_k, 0.0), axis=1
    ).astype(jnp.int32)
    column = jnp.arange(NX * 256, dtype=jnp.int32)
    x, inner = column // 256, column % 256
    energy = inner % 80 // 8 * 2 + inner // 80 - NW * ESTEP
    momentum = inner % 8
    chosen = (inner < COLS)[None, :] & (energy[None, :] == (2 * x)[None, :] + (b - shift)[:, None]) & (
        momentum[None, :] == reached[:, None]
    )
    return jnp.dot(spread, chosen.astype(jnp.bfloat16), preferred_element_type=jnp.bfloat16)


def kron_factors(grads):
    lane = jnp.arange(512, dtype=jnp.int32)
    taken = jnp.where(lane < 256, lane // 16, lane % 16)
    pick = (jnp.arange(NO, dtype=jnp.int32)[:, None] == taken[None, :]).astype(jnp.bfloat16)
    return jnp.dot(
        grads.reshape(BLOCK * NB * NO, NO), pick, preferred_element_type=jnp.float32
    )


def atoms_kernel(
    place_ref, below_ref, own_ref, above_ref, weights_ref, factors_ref, out_ref, lanes, near, sums
):
    done = 0
    for part in (below_ref, own_ref, above_ref):

        def widen(i, carry, part=part, done=done):
            rows = part[i].astype(jnp.float32)
            at = pl.multiple_of((done + i) * 72, 8)
            for half in range(2):
                lanes[half, pl.ds(at, 72), :] = rows[:, half * 128 : (half + 1) * 128]
            return carry

        lax.fori_loop(0, part.shape[0], widen, 0, unroll=4)
        done += part.shape[0]

    def regroup(atom, start, step):
        for b in range(2):
            for half in range(2):
                rows = lanes[half, pl.ds(start + b * step, 80, stride=72), :]
                near[atom, b * 80 : (b + 1) * 80, half * 128 : (half + 1) * 128] = rows.astype(
                    jnp.bfloat16
                )

    def regroup_atom(atom, carry):
        regroup(atom, atom, BLOCK)
        return carry

    lax.fori_loop(0, BLOCK, regroup_atom, 0, unroll=2)
    for h in range(2 * REACH):
        regroup(BLOCK + h, 2 * BLOCK + h, 2 * REACH)

    def one_atom(atom):
        total = jnp.zeros((64, 256), jnp.float32)
        for slot in range(NB):
            pair = atom * NB + slot
            row = pl.multiple_of(pair * 16, 16)
            band = jnp.concatenate(
                [weights_ref[pl.ds(row, 16), x * 256 : x * 256 + COLS] for x in range(NX)], axis=0
            )
            blended = jnp.dot(
                band, near[place_ref[pair]], preferred_element_type=jnp.float32
            ).astype(jnp.bfloat16)
            factors = factors_ref[pl.ds(row, 16), :]
            each, whole = factors[:, :256], factors[:, 256:]
            kron = jnp.concatenate(
                [(each[i : i + 1, :] * whole).astype(jnp.bfloat16) for i in range(NO)], axis=0
            )
            total = total + jnp.dot(blended, kron, preferred_element_type=jnp.float32)
        for half in range(2):
            sums[half, pl.ds(atom, 64, stride=BLOCK), :] = total[:, half * 128 : (half + 1) * 128]

    def some_atoms(step, carry):
        for i in range(UNROLL):
            one_atom(step * UNROLL + i)
        return carry

    lax.fori_loop(0, BLOCK // UNROLL, some_atoms, 0)

    def narrow(i, carry):
        at = pl.multiple_of(i * 64, 64)
        rows = [sums[half, pl.ds(at, 64), :] for half in range(2)]
        out_ref[i] = jnp.concatenate(rows, axis=1).astype(jnp.bfloat16)
        return carry

    lax.fori_loop(0, NX * NM, narrow, 0, unroll=4)


def self_energy_of(place, below, own, above, weights, factors):
    vmem = pl.BlockSpec(memory_space=pltpu.VMEM)
    flops = 2 * BLOCK * NB * 64 * (COLS + 256) * 256
    return pl.pallas_call(
        atoms_kernel,
        out_shape=jax.ShapeDtypeStruct((NX * NM, 2 * BLOCK, 256), jnp.bfloat16),
        in_specs=[pl.BlockSpec(memory_space=pltpu.SMEM)] + [vmem] * 5,
        out_specs=vmem,
        scratch_shapes=[
            pltpu.VMEM((2, 80 * 72, 128), jnp.float32),
            pltpu.VMEM((WIDE_BLOCK, COLS, 256), jnp.bfloat16),
            pltpu.VMEM((2, 2048, 128), jnp.float32),
        ],
        cost_estimate=pl.CostEstimate(flops=flops, bytes_accessed=16 << 20, transcendentals=0),
        compiler_params=pltpu.CompilerParams(vmem_limit_bytes=48 << 20),
    )(place, below, own, above, weights, factors)


def body(green_blocks, neighbours, counts, couplings, grad_h, momentum_table):
    own = group_exchange(packed_blocks(green_blocks.reshape(2, 1024, 256)))
    up = [(i, i + 1) for i in range(NZ - 1)]
    below = lax.ppermute(own[NM:], "z", up)
    above = lax.ppermute(own[:-NM], "z", [(b, a) for a, b in up])

    data = atom_data(neighbours, counts, couplings, grad_h)
    weights = banded_weights(data[:, 256:288], momentum_table)
    factors = kron_factors(data[:, :256])
    offset = data[:, 288].astype(jnp.float32).astype(jnp.int32)
    spot = jnp.arange(BLOCK * NB, dtype=jnp.int32) // NB + offset
    place = jnp.where(spot < 0, BLOCK + REACH + spot, jnp.where(spot < BLOCK, spot, REACH + spot))
    place = jnp.clip(place, 0, WIDE_BLOCK - 1)

    result = self_energy_of(place, below, own, above, weights, factors)
    back = group_exchange(result)
    back = back.reshape(NX, NM, 2, BLOCK, 256).transpose(2, 1, 0, 3, 4)
    return back.reshape(2, 1, 1024, 256)


def solution(mesh):
    cube = Mesh(mesh.devices.reshape(NZ, NX, NM), ("z", "x", "m"))
    flat = ("z", "x", "m")
    in_specs = (
        P(("z", "x"), "m", None, None),
        P(flat, None),
        P(flat),
        P(flat, None, None, None),
        P(flat, None, None, None),
        P(),
    )
    out_specs = P(("z", "x"), "m", None, None)
    return jax.shard_map(body, mesh=cube, in_specs=in_specs, out_specs=out_specs, check_vma=False)
```

time: 142 us -> 110 us (0.77)
  local copies, waits for them, and re-layouts: 38.4 us -> 5.15 us
  blocking collectives: 46.4 us -> 24.7 us
  Pallas kernels: 0 us -> 18.9 us
  waiting for transfers between devices: 8.77 us -> 23.3 us
  matrix products: 17.3 us -> 8.27 us
  other arithmetic: 8.45 us -> 6.46 us
    all_to_all x1, blocking collectives: 46.4 us -> 24.7 us  [group_exchange(): lax.all_to_all(blocks, ('x', 'm'), split_axis=0, concat_axis=0, tiled=True)]
    convert_element_type x1, local copies, waits for them, and re-layouts: 20.6 us -> 0.18 us  [atom_data(): jnp.where(used[:, :, None, None], couplings, 0.0).astype(jnp.bfloat16)]
    pallas_call x0 -> x2, Pallas kernels: none -> 18.9 us  [the longest x1 16.5 us: self_energy_of(): pl.pallas_call(atoms_kernel, out_shape=jax.ShapeDtypeStruct((NX * NM, 2 *...]
    dot_general x9 -> x3, matrix products: 17.3 us -> 8.27 us  [the longest x1 4.6 us: banded_weights(): jnp.dot(spread, chosen.astype(jnp.bfloat16), preferred_element_type=jnp.b...]
    ppermute x2 -> x3, waiting for transfers between devices: 5.6 us -> 13.3 us  [the longest x1 10.3 us: body(): above = lax.ppermute(own[:-NM], 'z', [(b, a) for a, b in up])]
    all_to_all x1 -> x2, waiting for transfers between devices: 3.18 us -> 9.97 us  [the longest x1 8.98 us: group_exchange(): lax.all_to_all(blocks, ('x', 'm'), split_axis=0, concat_axis=0, tiled=True)]
    another operation x8 -> x2, local copies, waits for them, and re-layouts: 4.82 us -> 0.16 us  [banded_weights(): tiled = jnp.tile(kept, (1, 2 * NM))]
    convert_element_type x2 -> x4, other arithmetic: 6.29 us -> 2.35 us  [the longest x1 0.84 us: atom_data(): jnp.where(used[:, :, None, None], couplings, 0.0).astype(jnp.bfloat16)]
  transfers between devices with their start and end apart: 3 -> 5, of which waited for: 3 -> 5; matrix products, arithmetic and copies ran while one was open for 20% -> 12% of each run, Pallas kernels for 0% -> 2%
where the time goes in v1:
time: 110 us; the launch traced here: 108 us
  blocking collectives  24.7 us (22%)
  waiting for transfers between devices  23.3 us (21%)
  starting transfers between devices  21.6 us (20%)
  Pallas kernels  18.9 us (17%)
  matrix products  8.27 us (8%)
  other arithmetic  6.46 us (6%)
  local copies, waits for them, and re-layouts  5.15 us (5%)
    all_to_all x1, blocking collectives, group_exchange(): lax.all_to_all(blocks, ('x', 'm'), split_axis=0, concat_axis=0, tiled=True)  24.7 us
    pallas_call x1, Pallas kernels, self_energy_of(): pl.pallas_call(atoms_kernel, out_shape=jax.ShapeDtypeStruct((NX * NM, 2 *...  16.5 us
    ppermute x1, waiting for transfers between devices, body(): above = lax.ppermute(own[:-NM], 'z', [(b, a) for a, b in up])  10.3 us
    all_to_all x1, waiting for transfers between devices, group_exchange(): lax.all_to_all(blocks, ('x', 'm'), split_axis=0, concat_axis=0, tiled=True)  8.98 us
    all_to_all x1, starting transfers between devices, atom_data(): lax.all_to_all(spread, 'm', split_axis=0, concat_axis=0, tiled=True)  6.46 us
    all_to_all x1, starting transfers between devices, group_exchange(): lax.all_to_all(blocks, ('x', 'm'), split_axis=0, concat_axis=0, tiled=True)  5.93 us
    dot_general x1, matrix products, banded_weights(): jnp.dot(spread, chosen.astype(jnp.bfloat16), preferred_element_type=jnp.b...  4.6 us
    ppermute x1, starting transfers between devices, body(): below = lax.ppermute(own[NM:], 'z', up)  4.22 us
  transfers between devices with their start and end apart: 5, of which 5 were waited for; matrix products, arithmetic and copies ran while one was open for 12% of the time, Pallas kernels for 2%

profile of v1, /device:TPU:1, one launch (start us, length us, event | category | flops | bytes accessed | tf_op | source)
XLA Modules:
  0.0 108.5 jit_solution(4751408018639918791)
XLA Ops:
  0.0 0.7 iota_compare_fusion.7
  0.7 0.8 subtract_convert_fusion
  1.6 1.0 reshape.268
  2.5 0.8 select_convert_fusion
  3.4 0.2 copy.16
  3.8 0.7 broadcast_in_dim.43
  4.5 6.5 %all-to-all-start = ((bf16[8,16,384]{2,1,0:T(8,128)(2,1)}), bf16[8,16,384]{2,1,0:T(8,128)(2,1)S(1)}, u32[]{:S(2)}, u32[]{:S(2)}) async-start(bf16[8,16,384]{2,1,0:T(8,128)(2,1)} %broadcast_in_dim.43), calls=%async_computation | async-start | bytes 196608 | tf_op jit(solution)/shard_map/all_to_all | solution.py:78
  10.9 1.0 fusion.5
  12.0 0.6 convert_element_type.35
  12.6 2.4 %shard_map.64 = bf16[32,72,256]{2,1,0:T(8,128)(2,1)} custom-call(bf16[2,1024,256]{2,1,0:T(8,128)(2,1)} %bitcast.16), custom_call_target="tpu_custom_call" | custom-call | flops 4194304 | bytes 2097152 | tf_op jit(solution)/shard_map/pallas_call | solution.py:51
  15.0 1.0 all-to-all-done
  15.9 5.9 %all-to-all-start.1 = ((bf16[32,72,256]{2,1,0:T(8,128)(2,1)}), bf16[32,72,256]{2,1,0:T(8,128)(2,1)S(1)}, u32[]{:S(2)}, u32[]{:S(2)}) async-start(bf16[32,72,256]{2,1,0:T(8,128)(2,1)} %shard_map.64), calls=%async_computation.1 | async-start | bytes 2359296 | tf_op jit(solution)/shard_map/all_to_all | solution.py:29
  21.9 0.6 fusion.39
  22.5 0.6 add_select_fusion
  23.1 3.7 %collective-permute-start = (bf16[8,16,384]{2,1,0:T(8,128)(2,1)S(1)}, bf16[8,16,384]{2,1,0:T(8,128)(2,1)S(1)}, u32[]{:S(2)}, u32[]{:S(2)}) collective-permute-start(bf16[8,16,384]{2,1,0:T(8,128)(2,1)S(1)} %all-to-all-done), channel_id=1, source_target_pairs={{0,0},{1,32},{2,64},{3,96},{4,128},{5,160},{6,192},{7,224},{32,1},... | collective-permute-start | bytes 294920 | tf_op jit(solution)/shard_map/ppermute | solution.py:80
  26.8 0.6 fusion.30
  27.4 2.0 %collective-permute-done = bf16[8,16,384]{2,1,0:T(8,128)(2,1)S(1)} collective-permute-done((bf16[8,16,384]{2,1,0:T(8,128)(2,1)S(1)}, bf16[8,16,384]{2,1,0:T(8,128)(2,1)S(1)}, u32[]{:S(2)}, u32[]{:S(2)}) %collective-permute-start) | collective-permute-done | bytes 98336 | tf_op jit(solution)/shard_map/ppermute | solution.py:80
  29.5 0.1 copy.19
  29.6 0.2 convert_reduce_fusion
  29.8 1.5 %broadcast_select_fusion = bf16[128,16,512]{2,1,0:T(8,128)(2,1)} fusion(pred[16,512]{1,0:T(8,128)(4,1)S(1)} %iota_compare_fusion.3, bf16[128,512]{1,0:T(8,128)(2,1)S(1)} %copy.19), kind=kLoop, calls=%fused_computation.5 | loop fusion | flops 1048576 | bytes 2236416 | tf_op jit(solution)/shard_map/jit(_where)/select_n | solution.py:87
  31.3 9.0 %all-to-all-done.1.own_ref = bf16[32,72,256]{2,1,0:T(8,128)(2,1)S(1)} async-done(((bf16[32,72,256]{2,1,0:T(8,128)(2,1)}), bf16[32,72,256]{2,1,0:T(8,128)(2,1)S(1)}, u32[]{:S(2)}, u32[]{:S(2)}) %all-to-all-start.1) | async-done | bytes 1179680 | tf_op jit(solution)/shard_map/all_to_all | solution.py:29
  40.2 1.4 %fusion.54 = (bf16[24,72,256]{2,1,0:T(8,128)(2,1)}, bf16[24,72,256]{2,1,0:T(8,128)(2,1)}) fusion(bf16[32,72,256]{2,1,0:T(8,128)(2,1)S(1)} %all-to-all-done.1.own_ref), kind=kLoop, calls=%fused_computation.108 | loop fusion | bytes 3538944 | tf_op jit(solution)/shard_map/slice | solution.py:210
  41.7 1.3 %collective-permute-start.2 = (bf16[24,72,256]{2,1,0:T(8,128)(2,1)}, bf16[24,72,256]{2,1,0:T(8,128)(2,1)S(1)}, u32[]{:S(2)}, u32[]{:S(2)}) collective-permute-start(bf16[24,72,256]{2,1,0:T(8,128)(2,1)} %get-tuple-element.5), channel_id=1, source_target_pairs={{32,0},{64,32},{96,64},{128,96},{160,128},{192,160},{224,192},{33,... | collective-permute-start | bytes 2654216 | tf_op jit(solution)/shard_map/ppermute | solution.py:210
  42.9 4.2 %collective-permute-start.1 = (bf16[24,72,256]{2,1,0:T(8,128)(2,1)}, bf16[24,72,256]{2,1,0:T(8,128)(2,1)S(1)}, u32[]{:S(2)}, u32[]{:S(2)}) collective-permute-start(bf16[24,72,256]{2,1,0:T(8,128)(2,1)} %get-tuple-element.6), channel_id=1, source_target_pairs={{0,32},{32,64},{64,96},{96,128},{128,160},{160,192},{192,224},{1,3... | collective-permute-start | bytes 2654216 | tf_op jit(solution)/shard_map/ppermute | solution.py:209
  47.2 0.4 reshape.273
  47.6 2.6 %fusion.13.factors_ref = f32[2048,512]{1,0:T(8,128)} fusion(bf16[2048,16]{1,0:T(8,128)(2,1)S(1)} %reshape.273, s32[512]{0:T(512)S(1)} %fusion.42), kind=kOutput, calls=%fused_computation.20 | convolution fusion | flops 33562624 | bytes 4261888 | tf_op jit(solution)/shard_map/dot_general | solution.py:115
  50.3 4.6 %fusion.2.weights_ref = bf16[2048,1024]{1,0:T(8,128)(2,1)} fusion(bf16[2048,512]{1,0:T(8,128)(2,1)S(1)} %bitcast.15, s32[1024]{0:T(1024)S(1)} %get-tuple-element.9, s32[512]{0:T(512)S(1)} %copy-done.3, s32[1024]{0:T(1024)S(1)} %fusion.20, s32[1024]{0:T(1024)S(1)} %copy-done.1, s32[512]{0:T(512)S(1)} %copy-done.2, pred[1024]{0:T(1024)(128)(4,1)S(1)} %copy-done.4), kind=kOutput, calls=%fused_computation.3 | convolution fusion | flops 2150105088 | bytes 6308864 | tf_op jit(solution)/shard_map/dot_general | solution.py:108
  54.9 10.3 %collective-permute-done.2.above_ref = bf16[24,72,256]{2,1,0:T(8,128)(2,1)S(1)} collective-permute-done((bf16[24,72,256]{2,1,0:T(8,128)(2,1)}, bf16[24,72,256]{2,1,0:T(8,128)(2,1)S(1)}, u32[]{:S(2)}, u32[]{:S(2)}) %collective-permute-start.2) | collective-permute-done | bytes 884768 | tf_op jit(solution)/shard_map/ppermute | solution.py:210
  65.2 1.0 collective-permute-done.1.below_ref
  66.2 16.5 %shard_map.65 = bf16[32,64,256]{2,1,0:T(8,128)(2,1)S(1)} custom-call(s32[128]{0:T(128)S(1)} %fusion.53.place_ref, bf16[24,72,256]{2,1,0:T(8,128)(2,1)S(1)} %collective-permute-done.1.below_ref, bf16[32,72,256]{2,1,0:T(8,128)(2,1)S(1)} %all-to-all-done.1.own_ref, bf16[24,72,256]{2,1,0:T(8,128)(2,1)S(1)} %collective-permute-done.2.above_ref, ...), custom_call_target="tpu_custom_call" | custom-call | flops 1744830464 | bytes 16777216 | tf_op jit(solution)/shard_map/pallas_call | solution.py:191
  82.7 24.7 %all_to_all.15 = bf16[32,64,256]{2,1,0:T(8,128)(2,1)S(1)} all-to-all(bf16[32,64,256]{2,1,0:T(8,128)(2,1)S(1)} %shard_map.65), channel_id=1, replica_groups=mesh['z'=8,'x'=4,'m'=8] {'x','m'}, dimensions={0} | all-to-all | bytes 2097152 | tf_op jit(solution)/shard_map/all_to_all | solution.py:29
  107.4 1.1 copy.20
  (26 shorter events, 0.5 us)
Async XLA Ops:
  4.5 11.5 %all-to-all-start = ((bf16[8,16,384]{2,1,0:T(8,128)(2,1)}), bf16[8,16,384]{2,1,0:T(8,128)(2,1)S(1)}, u32[]{:S(2)}, u32[]{:S(2)}) async-start(bf16[8,16,384]{2,1,0:T(8,128)(2,1)} %broadcast_in_dim.43), calls=%async_computation | async-start | bytes 196608 | tf_op jit(solution)/shard_map/all_to_all | solution.py:78
  15.9 24.3 %all-to-all-start.1 = ((bf16[32,72,256]{2,1,0:T(8,128)(2,1)}), bf16[32,72,256]{2,1,0:T(8,128)(2,1)S(1)}, u32[]{:S(2)}, u32[]{:S(2)}) async-start(bf16[32,72,256]{2,1,0:T(8,128)(2,1)} %shard_map.64), calls=%async_computation.1 | async-start | bytes 2359296 | tf_op jit(solution)/shard_map/all_to_all | solution.py:29
  23.1 6.3 %collective-permute-start = (bf16[8,16,384]{2,1,0:T(8,128)(2,1)S(1)}, bf16[8,16,384]{2,1,0:T(8,128)(2,1)S(1)}, u32[]{:S(2)}, u32[]{:S(2)}) collective-permute-start(bf16[8,16,384]{2,1,0:T(8,128)(2,1)S(1)} %all-to-all-done), channel_id=1, source_target_pairs={{0,0},{1,32},{2,64},{3,96},{4,128},{5,160},{6,192},{7,224},{32,1},... | collective-permute-start | bytes 294920 | tf_op jit(solution)/shard_map/ppermute | solution.py:80
  41.7 23.6 %collective-permute-start.2 = (bf16[24,72,256]{2,1,0:T(8,128)(2,1)}, bf16[24,72,256]{2,1,0:T(8,128)(2,1)S(1)}, u32[]{:S(2)}, u32[]{:S(2)}) collective-permute-start(bf16[24,72,256]{2,1,0:T(8,128)(2,1)} %get-tuple-element.5), channel_id=1, source_target_pairs={{32,0},{64,32},{96,64},{128,96},{160,128},{192,160},{224,192},{33,... | collective-permute-start | bytes 2654216 | tf_op jit(solution)/shard_map/ppermute | solution.py:210
  42.9 23.3 %collective-permute-start.1 = (bf16[24,72,256]{2,1,0:T(8,128)(2,1)}, bf16[24,72,256]{2,1,0:T(8,128)(2,1)S(1)}, u32[]{:S(2)}, u32[]{:S(2)}) collective-permute-start(bf16[24,72,256]{2,1,0:T(8,128)(2,1)} %get-tuple-element.6), channel_id=1, source_target_pairs={{0,32},{32,64},{64,96},{96,128},{128,160},{160,192},{192,224},{1,3... | collective-permute-start | bytes 2654216 | tf_op jit(solution)/shard_map/ppermute | solution.py:209
  47.6 2.7 %copy-start = (bf16[128,16,512]{2,1,0:T(8,128)(2,1)S(1)}, bf16[128,16,512]{2,1,0:T(8,128)(2,1)}, u32[]{:S(2)}) copy-start(bf16[128,16,512]{2,1,0:T(8,128)(2,1)} %broadcast_select_fusion) | copy-start | bytes 6291460
  47.6 2.7 %copy-start.1 = (s32[1024]{0:T(1024)S(1)}, s32[1024]{0:T(1024)}, u32[]{:S(2)}) copy-start(s32[1024]{0:T(1024)} %get-tuple-element.10) | copy-start | bytes 12292
  47.6 2.7 %copy-start.2 = (s32[512]{0:T(512)S(1)}, s32[512]{0:T(512)}, u32[]{:S(2)}) copy-start(s32[512]{0:T(512)} %convert_element_type.35) | copy-start | bytes 6148
  47.6 2.7 %copy-start.3 = (s32[512]{0:T(512)S(1)}, s32[512]{0:T(512)}, u32[]{:S(2)}) copy-start(s32[512]{0:T(512)} %fusion.39) | copy-start | bytes 6148
  47.6 2.7 %copy-start.4 = (pred[1024]{0:T(1024)(128)(4,1)S(1)}, pred[1024]{0:T(1024)(128)(4,1)}, u32[]{:S(2)}) copy-start(pred[1024]{0:T(1024)(128)(4,1)} %fusion.30) | copy-start | bytes 3076

commit v2 on v1

--- a/solution.py
+++ b/solution.py
@@ -1,11 +1,10 @@
-import functools
-
 import jax
 import jax.numpy as jnp
 from jax import lax
 from jax.experimental import pallas as pl
 from jax.experimental.pallas import tpu as pltpu
 from jax.sharding import Mesh, PartitionSpec as P
+
 
 REACH = 2
 NW = 2
@@ -18,11 +17,7 @@
 WIDE_BLOCK = BLOCK + 2 * REACH
 COLS = 160
 UNROLL = 2
-
-
-def shifts():
-    up = [(i + 1) * ESTEP for i in range(NW)]
-    return up + [-d for d in up]
+IN_STRIDE, OUT_STRIDE = 76, 36
 
 
 def group_exchange(blocks):
@@ -54,6 +49,7 @@
         in_specs=[vmem],
         out_specs=vmem,
         cost_estimate=pl.CostEstimate(flops=1 << 22, bytes_accessed=2 << 20, transcendentals=0),
+        compiler_params=pltpu.CompilerParams(vmem_limit_bytes=8 << 20),
     )(green)
 
 
@@ -74,10 +70,20 @@
         ],
         axis=1,
     )
-    spread = jnp.broadcast_to(rows[None], (NM, 16, 384))
-    spread = lax.all_to_all(spread, "m", split_axis=0, concat_axis=0, tiled=True)
-    swap = [(z * NM + m, m * NM + z) for z in range(NZ) for m in range(NM)]
-    return lax.ppermute(spread, ("z", "m"), swap).reshape(BLOCK * NB, 384)
+    held = rows[None]
+    for step in range(3):
+        pairs = [(z, z ^ (1 << step)) for z in range(NZ)]
+        held = jnp.concatenate([held, lax.ppermute(held, "z", pairs)], axis=0)
+    for step in range(3):
+        bit = (lax.axis_index("z") >> step) & 1
+        split = held.reshape(NZ >> (step + 1), 2, 1 << step, 16, 384)
+        held = jnp.where(bit == 1, jnp.flip(split, axis=1), split).reshape(NZ, 16, 384)
+    return held
+
+
+def group_data(held):
+    mine = lax.all_to_all(held, "m", split_axis=0, concat_axis=0, tiled=True)
+    return mine.reshape(BLOCK * NB, 384)
 
 
 def banded_weights(kept, momentum_table):
@@ -125,7 +131,7 @@
 
         def widen(i, carry, part=part, done=done):
             rows = part[i].astype(jnp.float32)
-            at = pl.multiple_of((done + i) * 72, 8)
+            at = pl.multiple_of((done + i) * IN_STRIDE, 4)
             for half in range(2):
                 lanes[half, pl.ds(at, 72), :] = rows[:, half * 128 : (half + 1) * 128]
             return carry
@@ -136,7 +142,7 @@
     def regroup(atom, start, step):
         for b in range(2):
             for half in range(2):
-                rows = lanes[half, pl.ds(start + b * step, 80, stride=72), :]
+                rows = lanes[half, pl.ds(start + b * step, 80, stride=IN_STRIDE), :]
                 near[atom, b * 80 : (b + 1) * 80, half * 128 : (half + 1) * 128] = rows.astype(
                     jnp.bfloat16
                 )
@@ -167,7 +173,7 @@
             )
             total = total + jnp.dot(blended, kron, preferred_element_type=jnp.float32)
         for half in range(2):
-            sums[half, pl.ds(atom, 64, stride=BLOCK), :] = total[:, half * 128 : (half + 1) * 128]
+            sums[half, pl.ds(atom, 64, stride=OUT_STRIDE), :] = total[:, half * 128 : (half + 1) * 128]
 
     def some_atoms(step, carry):
         for i in range(UNROLL):
@@ -177,9 +183,12 @@
     lax.fori_loop(0, BLOCK // UNROLL, some_atoms, 0)
 
     def narrow(i, carry):
-        at = pl.multiple_of(i * 64, 64)
-        rows = [sums[half, pl.ds(at, 64), :] for half in range(2)]
-        out_ref[i] = jnp.concatenate(rows, axis=1).astype(jnp.bfloat16)
+        for b in range(2):
+            at = pl.multiple_of((2 * i + b) * OUT_STRIDE, 4)
+            rows = [sums[half, pl.ds(at, BLOCK), :] for half in range(2)]
+            out_ref[i, b * BLOCK : (b + 1) * BLOCK, :] = jnp.concatenate(rows, axis=1).astype(
+                jnp.bfloat16
+            )
         return carry
 
     lax.fori_loop(0, NX * NM, narrow, 0, unroll=4)
@@ -194,26 +203,34 @@
         in_specs=[pl.BlockSpec(memory_space=pltpu.SMEM)] + [vmem] * 5,
         out_specs=vmem,
         scratch_shapes=[
-            pltpu.VMEM((2, 80 * 72, 128), jnp.float32),
+            pltpu.VMEM((2, 80 * IN_STRIDE, 128), jnp.float32),
             pltpu.VMEM((WIDE_BLOCK, COLS, 256), jnp.bfloat16),
-            pltpu.VMEM((2, 2048, 128), jnp.float32),
+            pltpu.VMEM((2, 64 * OUT_STRIDE, 128), jnp.float32),
         ],
         cost_estimate=pl.CostEstimate(flops=flops, bytes_accessed=16 << 20, transcendentals=0),
-        compiler_params=pltpu.CompilerParams(vmem_limit_bytes=48 << 20),
+        compiler_params=pltpu.CompilerParams(vmem_limit_bytes=24 << 20),
     )(place, below, own, above, weights, factors)
 
 
 def body(green_blocks, neighbours, counts, couplings, grad_h, momentum_table):
-    own = group_exchange(packed_blocks(green_blocks.reshape(2, 1024, 256)))
+    packed = packed_blocks(green_blocks.reshape(2, 1024, 256))
+    packed, neighbours, counts, couplings, grad_h = lax.optimization_barrier(
+        (packed, neighbours, counts, couplings, grad_h)
+    )
+    own = group_exchange(packed)
     up = [(i, i + 1) for i in range(NZ - 1)]
     below = lax.ppermute(own[NM:], "z", up)
     above = lax.ppermute(own[:-NM], "z", [(b, a) for a, b in up])
 
-    data = atom_data(neighbours, counts, couplings, grad_h)
+    held = atom_data(neighbours, counts, couplings, grad_h)
+    held, own = lax.optimization_barrier((held, own))
+    data = group_data(held)
     weights = banded_weights(data[:, 256:288], momentum_table)
     factors = kron_factors(data[:, :256])
     offset = data[:, 288].astype(jnp.float32).astype(jnp.int32)
-    spot = jnp.arange(BLOCK * NB, dtype=jnp.int32) // NB + offset
+    row = jnp.arange(BLOCK * NB, dtype=jnp.int32)
+    atom = row // NB
+    spot = atom + offset
     place = jnp.where(spot < 0, BLOCK + REACH + spot, jnp.where(spot < BLOCK, spot, REACH + spot))
     place = jnp.clip(place, 0, WIDE_BLOCK - 1)
 

time: 110 us -> 98.7 us (0.90); the launches traced: 108 us -> 98.3 us
  starting transfers between devices: 21.6 us -> 30.8 us
  waiting for transfers between devices: 23.3 us -> 15.5 us
  Pallas kernels: 18.9 us -> 12.6 us
  matrix products: 8.27 us -> 3.66 us
  other arithmetic: 6.46 us -> 5.03 us
    all_to_all x1, waiting for transfers between devices: 8.98 us -> 1.16 us  [group_exchange(): lax.all_to_all(blocks, ('x', 'm'), split_axis=0, concat_axis=0, tiled=True)]
    ppermute x1 -> x3, starting transfers between devices: 3.67 us -> 10.8 us  [atom_data(): held = jnp.concatenate([held, lax.ppermute(held, 'z', pairs)], axis=0)]
    pallas_call x1, Pallas kernels: 16.5 us -> 11.4 us  [self_energy_of(): pl.pallas_call(atoms_kernel, out_shape=jax.ShapeDtypeStruct((NX * NM, 2 *...]
    all_to_all x1, starting transfers between devices: 5.93 us -> 8.58 us  [group_exchange(): lax.all_to_all(blocks, ('x', 'm'), split_axis=0, concat_axis=0, tiled=True)]
    unnamed x10 -> x22, local copies, waits for them, and re-layouts: 0.02 us -> 2.12 us
    dot_general x1, matrix products: 4.6 us -> 2.63 us  [banded_weights(): jnp.dot(spread, chosen.astype(jnp.bfloat16), preferred_element_type=jnp.b...]
    dot_general x1, matrix products: 2.63 us -> 0.68 us  [kron_factors(): jnp.dot(grads.reshape(BLOCK * NB * NO, NO), pick, preferred_element_type=...]
    pallas_call x1, Pallas kernels: 2.38 us -> 1.18 us  [packed_blocks(): pl.pallas_call(pack_kernel, out_shape=jax.ShapeDtypeStruct((NX * NM, 2 *...]
  transfers between devices with their start and end apart: 5 -> 7, of which waited for: 5 -> 6; matrix products, arithmetic and copies ran while one was open for 12% -> 11% of each run, Pallas kernels for 2% -> 0%
where the time goes in v2:
time: 98.7 us; the launch traced here: 98.3 us
  starting transfers between devices  30.8 us (31%)
  blocking collectives  24.8 us (25%)
  waiting for transfers between devices  15.5 us (16%)
  Pallas kernels  12.6 us (13%)
  local copies, waits for them, and re-layouts  5.68 us (6%)
  other arithmetic  5.03 us (5%)
  matrix products  3.66 us (4%)
    all_to_all x1, blocking collectives, group_exchange(): lax.all_to_all(blocks, ('x', 'm'), split_axis=0, concat_axis=0, tiled=True)  24.8 us
    pallas_call x1, Pallas kernels, self_energy_of(): pl.pallas_call(atoms_kernel, out_shape=jax.ShapeDtypeStruct((NX * NM, 2 *...  11.4 us
    ppermute x1, waiting for transfers between devices, body(): above = lax.ppermute(own[:-NM], 'z', [(b, a) for a, b in up])  11.4 us
    ppermute x3, starting transfers between devices, atom_data(): held = jnp.concatenate([held, lax.ppermute(held, 'z', pairs)], axis=0)  10.8 us
    all_to_all x1, starting transfers between devices, group_exchange(): lax.all_to_all(blocks, ('x', 'm'), split_axis=0, concat_axis=0, tiled=True)  8.58 us
    all_to_all x1, starting transfers between devices, group_data(): mine = lax.all_to_all(held, 'm', split_axis=0, concat_axis=0, tiled=True)  6.04 us
    ppermute x1, starting transfers between devices, body(): below = lax.ppermute(own[NM:], 'z', up)  4.04 us
    dot_general x1, matrix products, banded_weights(): jnp.dot(spread, chosen.astype(jnp.bfloat16), preferred_element_type=jnp.b...  2.63 us
  transfers between devices with their start and end apart: 7, of which 6 were waited for; matrix products, arithmetic and copies ran while one was open for 11% of the time, Pallas kernels for 0%

profile of v2, /device:TPU:1, one launch (start us, length us, event | category | flops | bytes accessed | tf_op | source)
XLA Modules:
  0.0 98.3 jit_solution(16163537307394983851)
XLA Ops:
  0.0 1.2 %copy-done = bf16[2,1,1024,256]{3,2,1,0:T(8,128)(2,1)S(1)} copy-done((bf16[2,1,1024,256]{3,2,1,0:T(8,128)(2,1)S(1)}, bf16[2,1,1024,256]{3,2,1,0:T(8,128)(2,1)}, u32[]{:S(2)}) %copy-start) | copy-done | bytes 1048600
  1.2 1.2 %shard_map.64 = bf16[32,72,256]{2,1,0:T(8,128)(2,1)} custom-call(bf16[2,1024,256]{2,1,0:T(8,128)(2,1)S(1)} %bitcast.20), custom_call_target="tpu_custom_call" | custom-call | flops 4194304 | bytes 2097152 | tf_op jit(solution)/shard_map/pallas_call | solution.py:46
  2.4 8.6 %all-to-all-start = ((bf16[32,72,256]{2,1,0:T(8,128)(2,1)}), bf16[32,72,256]{2,1,0:T(8,128)(2,1)S(1)}, u32[]{:S(2)}, u32[]{:S(2)}) async-start(bf16[32,72,256]{2,1,0:T(8,128)(2,1)} %shard_map.64), calls=%async_computation | async-start | bytes 2359296 | tf_op jit(solution)/shard_map/all_to_all | solution.py:24
  11.5 0.2 copy.16
  11.9 1.7 %collective-permute-start = (bf16[1,16,384]{2,1,0:T(8,128)(2,1)S(1)}, bf16[1,16,384]{2,1,0:T(8,128)(2,1)S(1)}, u32[]{:S(2)}, u32[]{:S(2)}) collective-permute-start(bf16[1,16,384]{2,1,0:T(8,128)(2,1)S(1)} %maximum_bitcast_fusion), channel_id=1, source_target_pairs={{0,32},{32,0},{64,96},{96,64},{128,160},{160,128},{192,224},{224,1... | collective-permute-start | bytes 36872 | tf_op jit(solution)/shard_map/ppermute | solution.py:76
  13.6 0.6 add_select_fusion
  14.2 0.3 fusion.5
  14.6 0.4 collective-permute-done
  15.0 3.0 %collective-permute-start.1 = (bf16[2,16,384]{2,1,0:T(8,128)(2,1)S(1)}, bf16[2,16,384]{2,1,0:T(8,128)(2,1)S(1)}, u32[]{:S(2)}, u32[]{:S(2)}) collective-permute-start(bf16[2,16,384]{2,1,0:T(8,128)(2,1)S(1)} %pad_maximum_fusion.2), channel_id=1, source_target_pairs={{0,64},{32,96},{64,0},{96,32},{128,192},{160,224},{192,128},{224,1... | collective-permute-start | bytes 73736 | tf_op jit(solution)/shard_map/ppermute | solution.py:76
  18.0 0.5 fusion.39
  18.5 1.0 collective-permute-done.1
  19.5 6.2 %collective-permute-start.2 = (bf16[4,16,384]{2,1,0:T(8,128)(2,1)S(1)}, bf16[4,16,384]{2,1,0:T(8,128)(2,1)S(1)}, u32[]{:S(2)}, u32[]{:S(2)}) collective-permute-start(bf16[4,16,384]{2,1,0:T(8,128)(2,1)S(1)} %pad_maximum_fusion.1), channel_id=1, source_target_pairs={{0,128},{32,160},{64,192},{96,224},{128,0},{160,32},{192,64},{224,... | collective-permute-start | bytes 147464 | tf_op jit(solution)/shard_map/ppermute | solution.py:76
  25.7 0.5 fusion.30
  26.2 0.6 convert_element_type.35
  26.8 0.7 collective-permute-done.2
  27.6 0.7 reverse_select_fusion
  28.2 1.2 %all-to-all-done.own_ref = bf16[32,72,256]{2,1,0:T(8,128)(2,1)S(1)} async-done(((bf16[32,72,256]{2,1,0:T(8,128)(2,1)}), bf16[32,72,256]{2,1,0:T(8,128)(2,1)S(1)}, u32[]{:S(2)}, u32[]{:S(2)}) %all-to-all-start) | async-done | bytes 1179680 | tf_op jit(solution)/shard_map/all_to_all | solution.py:24
  29.4 6.0 %all-to-all-start.1 = ((bf16[8,16,384]{2,1,0:T(8,128)(2,1)}), bf16[8,16,384]{2,1,0:T(8,128)(2,1)S(1)}, u32[]{:S(2)}, u32[]{:S(2)}) async-start(bf16[8,16,384]{2,1,0:T(8,128)(2,1)} %bitcast.5), calls=%async_computation.1 | async-start | bytes 196608 | tf_op jit(solution)/shard_map/all_to_all | solution.py:85
  35.4 1.3 %fusion.54 = (bf16[24,72,256]{2,1,0:T(8,128)(2,1)}, bf16[24,72,256]{2,1,0:T(8,128)(2,1)}) fusion(bf16[32,72,256]{2,1,0:T(8,128)(2,1)S(1)} %all-to-all-done.own_ref), kind=kLoop, calls=%fused_computation.114 | loop fusion | bytes 3538944 | tf_op jit(solution)/shard_map/slice | solution.py:223
  36.7 1.3 %collective-permute-start.4 = (bf16[24,72,256]{2,1,0:T(8,128)(2,1)}, bf16[24,72,256]{2,1,0:T(8,128)(2,1)S(1)}, u32[]{:S(2)}, u32[]{:S(2)}) collective-permute-start(bf16[24,72,256]{2,1,0:T(8,128)(2,1)} %get-tuple-element.19), channel_id=1, source_target_pairs={{32,0},{64,32},{96,64},{128,96},{160,128},{192,160},{224,192},{33,... | collective-permute-start | bytes 2654216 | tf_op jit(solution)/shard_map/ppermute | solution.py:223
  38.0 4.0 %collective-permute-start.3 = (bf16[24,72,256]{2,1,0:T(8,128)(2,1)}, bf16[24,72,256]{2,1,0:T(8,128)(2,1)S(1)}, u32[]{:S(2)}, u32[]{:S(2)}) collective-permute-start(bf16[24,72,256]{2,1,0:T(8,128)(2,1)} %get-tuple-element.20), channel_id=1, source_target_pairs={{0,32},{32,64},{64,96},{96,128},{128,160},{160,192},{192,224},{1,3... | collective-permute-start | bytes 2654216 | tf_op jit(solution)/shard_map/ppermute | solution.py:222
  42.1 0.2 convert_reduce_fusion
  42.5 1.5 %broadcast_select_fusion = bf16[128,16,512]{2,1,0:T(8,128)(2,1)} fusion(pred[16,512]{1,0:T(8,128)(4,1)S(1)} %iota_compare_fusion.3, bf16[128,512]{1,0:T(8,128)(2,1)S(1)} %copy.19), kind=kLoop, calls=%fused_computation.5 | loop fusion | flops 1048576 | bytes 2236416 | tf_op jit(solution)/shard_map/jit(_where)/select_n | solution.py:93
  44.0 0.4 reshape.280
  44.5 0.7 fusion.13.factors_ref
  45.2 0.9 copy-done.1
  46.0 2.6 %fusion.2.weights_ref = bf16[2048,1024]{1,0:T(8,128)(2,1)S(1)} fusion(bf16[2048,512]{1,0:T(8,128)(2,1)S(1)} %bitcast.22, s32[1024]{0:T(1024)S(1)} %get-tuple-element.23, s32[512]{0:T(512)S(1)} %copy-done.6, s32[1024]{0:T(1024)S(1)} %fusion.20, s32[1024]{0:T(1024)S(1)} %copy-done.4, s32[512]{0:T(512)S(1)} %copy-done.7, pred[1024]{0:T(1024)(128)(4,1)S(1)} %copy-done.10), kind=kOutput, calls=%fused_computation.3 | convolution fusion | flops 2150105088 | bytes 6308864 | tf_op jit(solution)/shard_map/dot_general | solution.py:114
  48.7 11.4 %collective-permute-done.4.above_ref = bf16[24,72,256]{2,1,0:T(8,128)(2,1)S(1)} collective-permute-done((bf16[24,72,256]{2,1,0:T(8,128)(2,1)}, bf16[24,72,256]{2,1,0:T(8,128)(2,1)S(1)}, u32[]{:S(2)}, u32[]{:S(2)}) %collective-permute-start.4) | collective-permute-done | bytes 884768 | tf_op jit(solution)/shard_map/ppermute | solution.py:223
  60.0 1.0 %collective-permute-done.3.below_ref = bf16[24,72,256]{2,1,0:T(8,128)(2,1)S(1)} collective-permute-done((bf16[24,72,256]{2,1,0:T(8,128)(2,1)}, bf16[24,72,256]{2,1,0:T(8,128)(2,1)S(1)}, u32[]{:S(2)}, u32[]{:S(2)}) %collective-permute-start.3) | collective-permute-done | bytes 884768 | tf_op jit(solution)/shard_map/ppermute | solution.py:222
  61.0 11.4 %shard_map.65 = bf16[32,64,256]{2,1,0:T(8,128)(2,1)S(1)} custom-call(s32[128]{0:T(128)S(1)} %fusion.53.place_ref, bf16[24,72,256]{2,1,0:T(8,128)(2,1)S(1)} %collective-permute-done.3.below_ref, bf16[32,72,256]{2,1,0:T(8,128)(2,1)S(1)} %all-to-all-done.own_ref, bf16[24,72,256]{2,1,0:T(8,128)(2,1)S(1)} %collective-permute-done.4.above_ref, ...), custom_call_target="tpu_custom_call" | custom-call | flops 1744830464 | bytes 16777216 | tf_op jit(solution)/shard_map/pallas_call | solution.py:200
  72.4 24.8 %all_to_all.15 = bf16[32,64,256]{2,1,0:T(8,128)(2,1)S(1)} all-to-all(bf16[32,64,256]{2,1,0:T(8,128)(2,1)S(1)} %shard_map.65), channel_id=1, replica_groups=mesh['z'=8,'x'=4,'m'=8] {'x','m'}, dimensions={0} | all-to-all | bytes 2097152 | tf_op jit(solution)/shard_map/all_to_all | solution.py:24
  97.3 1.1 %copy.20 = bf16[2,8,4,32,256]{4,3,2,1,0:T(8,128)(2,1)} copy(bf16[2,8,4,32,256]{4,3,0,1,2:T(8,128)(2,1)S(1)} %bitcast.21) | data formatting | bytes 2097152 | tf_op jit(solution)/shard_map/transpose | solution.py:239
  (47 shorter events, 1.1 us)
Async XLA Ops:
  0.0 1.2 %copy-start = (bf16[2,1,1024,256]{3,2,1,0:T(8,128)(2,1)S(1)}, bf16[2,1,1024,256]{3,2,1,0:T(8,128)(2,1)}, u32[]{:S(2)}) copy-start(bf16[2,1,1024,256]{3,2,1,0:T(8,128)(2,1)} %param.6) | copy-start | bytes 3145732
  1.2 9.8 %copy-start.9 = (s32[4]{0:T(128)S(1)}, s32[4]{0:T(128)}, u32[]{:S(2)}) copy-start(s32[4]{0:T(128)} %param.8) | copy-start | bytes 52
  1.2 9.9 %copy-start.5 = (s32[4,4]{1,0:T(4,128)S(1)}, s32[4,4]{1,0:T(4,128)}, u32[]{:S(2)}) copy-start(s32[4,4]{1,0:T(4,128)} %param.7) | copy-start | bytes 196
  1.2 10.0 %copy-start.2 = (bf16[4,4,16,16]{3,2,1,0:T(8,128)(2,1)S(1)}, bf16[4,4,16,16]{3,2,1,0:T(8,128)(2,1)}, u32[]{:S(2)}) copy-start(bf16[4,4,16,16]{3,2,1,0:T(8,128)(2,1)} %param.10) | copy-start | bytes 24580
  1.2 10.2 %copy-start.3 = (f32[4,4,8,4]{2,3,1,0:T(4,128)S(1)}, f32[4,4,8,4]{2,3,1,0:T(4,128)}, u32[]{:S(2)}) copy-start(f32[4,4,8,4]{2,3,1,0:T(4,128)} %param.9) | copy-start | bytes 6148
  1.2 13.0 %copy-start.8 = (s32[8,8]{1,0:T(8,128)S(1)}, s32[8,8]{1,0:T(8,128)}, u32[]{:S(2)}) copy-start(s32[8,8]{1,0:T(8,128)} %param.11) | copy-start | bytes 772
  2.4 26.9 %all-to-all-start = ((bf16[32,72,256]{2,1,0:T(8,128)(2,1)}), bf16[32,72,256]{2,1,0:T(8,128)(2,1)S(1)}, u32[]{:S(2)}, u32[]{:S(2)}) async-start(bf16[32,72,256]{2,1,0:T(8,128)(2,1)} %shard_map.64), calls=%async_computation | async-start | bytes 2359296 | tf_op jit(solution)/shard_map/all_to_all | solution.py:24
  11.9 3.0 %collective-permute-start = (bf16[1,16,384]{2,1,0:T(8,128)(2,1)S(1)}, bf16[1,16,384]{2,1,0:T(8,128)(2,1)S(1)}, u32[]{:S(2)}, u32[]{:S(2)}) collective-permute-start(bf16[1,16,384]{2,1,0:T(8,128)(2,1)S(1)} %maximum_bitcast_fusion), channel_id=1, source_target_pairs={{0,32},{32,0},{64,96},{96,64},{128,160},{160,128},{192,224},{224,1... | collective-permute-start | bytes 36872 | tf_op jit(solution)/shard_map/ppermute | solution.py:76
  15.0 4.5 %collective-permute-start.1 = (bf16[2,16,384]{2,1,0:T(8,128)(2,1)S(1)}, bf16[2,16,384]{2,1,0:T(8,128)(2,1)S(1)}, u32[]{:S(2)}, u32[]{:S(2)}) collective-permute-start(bf16[2,16,384]{2,1,0:T(8,128)(2,1)S(1)} %pad_maximum_fusion.2), channel_id=1, source_target_pairs={{0,64},{32,96},{64,0},{96,32},{128,192},{160,224},{192,128},{224,1... | collective-permute-start | bytes 73736 | tf_op jit(solution)/shard_map/ppermute | solution.py:76
  19.5 8.0 %collective-permute-start.2 = (bf16[4,16,384]{2,1,0:T(8,128)(2,1)S(1)}, bf16[4,16,384]{2,1,0:T(8,128)(2,1)S(1)}, u32[]{:S(2)}, u32[]{:S(2)}) collective-permute-start(bf16[4,16,384]{2,1,0:T(8,128)(2,1)S(1)} %pad_maximum_fusion.1), channel_id=1, source_target_pairs={{0,128},{32,160},{64,192},{96,224},{128,0},{160,32},{192,64},{224,... | collective-permute-start | bytes 147464 | tf_op jit(solution)/shard_map/ppermute | solution.py:76
  29.4 12.7 %all-to-all-start.1 = ((bf16[8,16,384]{2,1,0:T(8,128)(2,1)}), bf16[8,16,384]{2,1,0:T(8,128)(2,1)S(1)}, u32[]{:S(2)}, u32[]{:S(2)}) async-start(bf16[8,16,384]{2,1,0:T(8,128)(2,1)} %bitcast.5), calls=%async_computation.1 | async-start | bytes 196608 | tf_op jit(solution)/shard_map/all_to_all | solution.py:85
  36.7 23.3 %collective-permute-start.4 = (bf16[24,72,256]{2,1,0:T(8,128)(2,1)}, bf16[24,72,256]{2,1,0:T(8,128)(2,1)S(1)}, u32[]{:S(2)}, u32[]{:S(2)}) collective-permute-start(bf16[24,72,256]{2,1,0:T(8,128)(2,1)} %get-tuple-element.19), channel_id=1, source_target_pairs={{32,0},{64,32},{96,64},{128,96},{160,128},{192,160},{224,192},{33,... | collective-permute-start | bytes 2654216 | tf_op jit(solution)/shard_map/ppermute | solution.py:223
  38.0 23.0 %collective-permute-start.3 = (bf16[24,72,256]{2,1,0:T(8,128)(2,1)}, bf16[24,72,256]{2,1,0:T(8,128)(2,1)S(1)}, u32[]{:S(2)}, u32[]{:S(2)}) collective-permute-start(bf16[24,72,256]{2,1,0:T(8,128)(2,1)} %get-tuple-element.20), channel_id=1, source_target_pairs={{0,32},{32,64},{64,96},{96,128},{128,160},{160,192},{192,224},{1,3... | collective-permute-start | bytes 2654216 | tf_op jit(solution)/shard_map/ppermute | solution.py:222
  44.4 1.6 %copy-start.1 = (bf16[128,16,512]{2,1,0:T(8,128)(2,1)S(1)}, bf16[128,16,512]{2,1,0:T(8,128)(2,1)}, u32[]{:S(2)}) copy-start(bf16[128,16,512]{2,1,0:T(8,128)(2,1)} %broadcast_select_fusion) | copy-start | bytes 6291460
  44.4 1.6 %copy-start.4 = (s32[1024]{0:T(1024)S(1)}, s32[1024]{0:T(1024)}, u32[]{:S(2)}) copy-start(s32[1024]{0:T(1024)} %get-tuple-element.24) | copy-start | bytes 12292
  44.4 1.6 %copy-start.6 = (s32[512]{0:T(512)S(1)}, s32[512]{0:T(512)}, u32[]{:S(2)}) copy-start(s32[512]{0:T(512)} %fusion.39) | copy-start | bytes 6148
  44.4 1.6 %copy-start.7 = (s32[512]{0:T(512)S(1)}, s32[512]{0:T(512)}, u32[]{:S(2)}) copy-start(s32[512]{0:T(512)} %convert_element_type.35) | copy-start | bytes 6148
  44.5 1.6 %copy-start.10 = (pred[1024]{0:T(1024)(128)(4,1)S(1)}, pred[1024]{0:T(1024)(128)(4,1)}, u32[]{:S(2)}) copy-start(pred[1024]{0:T(1024)(128)(4,1)} %fusion.30) | copy-start | bytes 3076

commit v3 on v2

v3 whole, which is shorter than its diff:
```python
import jax
import jax.numpy as jnp
from jax import lax
from jax.experimental import pallas as pl
from jax.experimental.pallas import tpu as pltpu
from jax.sharding import Mesh, PartitionSpec as P


REACH = 2
NW = 2
ESTEP = 3

NZ, NX, NM = 8, 4, 8
NO = 16
NB = 4
BLOCK = 32
WIDE_BLOCK = BLOCK + 2 * REACH
COLS = 160
UNROLL = 2
IN_STRIDE, OUT_STRIDE = 76, 34
OFFSETS = (-2, -1, 1, 2)
CHUNK = 32


def group_exchange(blocks):
    return lax.all_to_all(blocks, ("x", "m"), split_axis=0, concat_axis=0, tiled=True)


def pack_kernel(green_ref, out_ref):
    for m in range(NM):
        for x in range(NX):
            first = (m * NX + x) * BLOCK
            dest = x * NM + m
            halo = []
            for b in range(2):
                out_ref[dest, b * BLOCK : (b + 1) * BLOCK, :] = green_ref[
                    b, first : first + BLOCK, :
                ]
                left = green_ref[b, max(first - 16, 0) : max(first - 16, 0) + 16, :][16 - REACH :]
                after = min(first + BLOCK, 1024 - 16)
                right = green_ref[b, after : after + 16, :][:REACH]
                halo += [left, right]
            out_ref[dest, 2 * BLOCK :, :] = jnp.concatenate(halo, axis=0)


def packed_blocks(green):
    vmem = pl.BlockSpec(memory_space=pltpu.VMEM)
    return pl.pallas_call(
        pack_kernel,
        out_shape=jax.ShapeDtypeStruct((NX * NM, 2 * WIDE_BLOCK, 256), green.dtype),
        in_specs=[vmem],
        out_specs=vmem,
        cost_estimate=pl.CostEstimate(flops=1 << 22, bytes_accessed=2 << 20, transcendentals=0),
        compiler_params=pltpu.CompilerParams(vmem_limit_bytes=8 << 20),
    )(green)


def atom_data(neighbours, counts, couplings, grad_h):
    start = 4 * (
        (lax.axis_index("z") * NX + lax.axis_index("x")) * NM + lax.axis_index("m")
    )
    atoms = start + jnp.arange(4, dtype=jnp.int32)
    used = jnp.arange(NB, dtype=jnp.int32)[None, :] < counts[:, None]
    offset = jnp.where(used, neighbours - atoms[:, None], 0)
    wanted = jnp.arange(NB, dtype=jnp.int32) - 2
    wanted = jnp.where(wanted < 0, wanted, wanted + 1)
    here = (offset[:, None, :] == wanted[None, :, None])[..., None, None]
    kept = jnp.sum(jnp.where(here, couplings[:, None], 0.0), axis=2)
    grads = jnp.sum(jnp.where(here, grad_h[:, None].astype(jnp.float32), 0.0), axis=2)
    kept = kept.astype(jnp.bfloat16).reshape(16, 32)
    grads = grads.astype(jnp.bfloat16).reshape(16, 256)
    rows = jnp.concatenate([grads, jnp.tile(kept, (1, NM))], axis=1)
    held = rows[None]
    for step in range(3):
        pairs = [(z, z ^ (1 << step)) for z in range(NZ)]
        held = jnp.concatenate([held, lax.ppermute(held, "z", pairs)], axis=0)
    return held


def sort_kernel(held_ref, out_ref):
    z = lax.axis_index("z")
    for piece in range(NZ):
        out_ref[piece] = held_ref[jnp.bitwise_xor(z, piece)]


def sorted_pieces(held):
    vmem = pl.BlockSpec(memory_space=pltpu.VMEM)
    return pl.pallas_call(
        sort_kernel,
        out_shape=jax.ShapeDtypeStruct(held.shape, held.dtype),
        in_specs=[vmem],
        out_specs=vmem,
        cost_estimate=pl.CostEstimate(flops=1 << 18, bytes_accessed=1 << 18, transcendentals=0),
        compiler_params=pltpu.CompilerParams(vmem_limit_bytes=2 << 20),
    )(held)


def group_data(held):
    mine = lax.all_to_all(sorted_pieces(held), "m", split_axis=0, concat_axis=0, tiled=True)
    return mine.reshape(BLOCK * NB, 512)


def choice_kernel(table_ref, out_ref):
    shape = (32, 512)
    row = lax.broadcasted_iota(jnp.int32, shape, 0)
    column = lax.broadcasted_iota(jnp.int32, shape, 1)
    q, s = row // 4, row % 4
    shift = jnp.where(s < NW, (s + 1) * ESTEP, (NW - 1 - s) * ESTEP)
    inner = column % 256
    energy = inner % 80 // 8 * 2 + inner // 80 - NW * ESTEP
    aim = jnp.where(inner < COLS, energy - column // 256 + shift, -100)
    for k in range(NM):
        reached = jnp.zeros(shape, jnp.int32)
        for place in range(NM):
            reached = jnp.where(q == place, table_ref[k, place], reached)
        same = inner % 8 == reached
        for x in range(NX):
            chosen = jnp.where(same & (aim == 2 * x), 1.0, 0.0)
            out_ref[k * 32 : (k + 1) * 32, x * 512 : (x + 1) * 512] = chosen.astype(jnp.bfloat16)


def column_choice(momentum_table):
    return pl.pallas_call(
        choice_kernel,
        out_shape=jax.ShapeDtypeStruct((NM * 32, NX * 512), jnp.bfloat16),
        in_specs=[pl.BlockSpec(memory_space=pltpu.SMEM)],
        out_specs=pl.BlockSpec(memory_space=pltpu.VMEM),
        cost_estimate=pl.CostEstimate(flops=1 << 24, bytes_accessed=1 << 20, transcendentals=0),
        compiler_params=pltpu.CompilerParams(vmem_limit_bytes=4 << 20),
    )(momentum_table)


def weights_kernel(data_ref, choice_ref, out_ref, factors_ref):
    lane = lax.broadcasted_iota(jnp.int32, (NM, 256), 1)
    mine = lane // 32 == lax.broadcasted_iota(jnp.int32, (NM, 256), 0)
    lane = lax.broadcasted_iota(jnp.int32, (NO, 256), 1)
    in_row = lane // NO == lax.broadcasted_iota(jnp.int32, (NO, 256), 0)
    entry = lax.broadcasted_iota(jnp.int32, (256, 512), 0) % NO
    lane = lax.broadcasted_iota(jnp.int32, (256, 512), 1)
    taken = jnp.where(lane < 256, lane // NO, lane % NO)
    pick = jnp.where(entry == taken, 1.0, 0.0).astype(jnp.bfloat16)

    def some_pairs(step, carry):
        at = pl.multiple_of(step * CHUNK, CHUNK)
        kept = data_ref[pl.ds(at, CHUNK), 256:512].astype(jnp.float32)
        rows = [jnp.where(mine, kept[i : i + 1, :], 0.0) for i in range(CHUNK)]
        spread = jnp.concatenate(rows, axis=0).astype(jnp.bfloat16)
        for x in range(NX):
            both = [
                jnp.dot(
                    spread,
                    choice_ref[:, (2 * x + b) * 256 : (2 * x + b + 1) * 256],
                    preferred_element_type=jnp.float32,
                ).reshape(CHUNK, NM, 256)
                for b in range(2)
            ]
            out_ref[pl.ds(at, CHUNK), x * 16 : (x + 1) * 16, :] = jnp.concatenate(
                both, axis=1
            ).astype(jnp.bfloat16)
        grads = data_ref[pl.ds(at, CHUNK), :256].astype(jnp.float32)
        rows = [jnp.where(in_row, grads[i : i + 1, :], 0.0) for i in range(CHUNK)]
        factors_ref[pl.ds(pl.multiple_of(at * NO, CHUNK * NO), CHUNK * NO), :] = jnp.dot(
            jnp.concatenate(rows, axis=0).astype(jnp.bfloat16),
            pick,
            preferred_element_type=jnp.float32,
        )
        return carry

    lax.fori_loop(0, BLOCK * NB // CHUNK, some_pairs, 0)


def weights_and_factors(data, choice):
    vmem = pl.BlockSpec(memory_space=pltpu.VMEM)
    return pl.pallas_call(
        weights_kernel,
        out_shape=[
            jax.ShapeDtypeStruct((BLOCK * NB, 64, 256), jnp.bfloat16),
            jax.ShapeDtypeStruct((BLOCK * NB * NO, 512), jnp.float32),
        ],
        in_specs=[vmem, vmem],
        out_specs=[vmem, vmem],
        cost_estimate=pl.CostEstimate(flops=1 << 30, bytes_accessed=6 << 20, transcendentals=0),
        compiler_params=pltpu.CompilerParams(vmem_limit_bytes=16 << 20),
    )(data, choice)


def atoms_kernel(
    below_ref, own_ref, above_ref, weights_ref, factors_ref, out_ref, lanes, near, blend, sums
):
    done = 0
    for part in (below_ref, own_ref, above_ref):

        def widen(i, carry, part=part, done=done):
            rows = part[i].astype(jnp.float32)
            at = pl.multiple_of((done + i) * IN_STRIDE, 4)
            for half in range(2):
                lanes[half, pl.ds(at, 72), :] = rows[:, half * 128 : (half + 1) * 128]
            return carry

        lax.fori_loop(0, part.shape[0], widen, 0, unroll=4)
        done += part.shape[0]

    def regroup(place, start, step):
        for b in range(2):
            for half in range(2):
                rows = lanes[half, pl.ds(start + b * step, 80, stride=IN_STRIDE), :]
                near[place, b * 80 : (b + 1) * 80, half * 128 : (half + 1) * 128] = rows.astype(
                    jnp.bfloat16
                )

    def regroup_atom(atom, carry):
        regroup(REACH + atom, atom, BLOCK)
        return carry

    lax.fori_loop(0, BLOCK, regroup_atom, 0, unroll=2)
    for h in range(2 * REACH):
        regroup(h if h < REACH else BLOCK + h, 2 * BLOCK + h, 2 * REACH)

    def blend_from(place, carry):
        bands = []
        for d, offset in enumerate(OFFSETS):
            atom = jnp.clip(place - REACH - offset, 0, BLOCK - 1)
            bands.append(weights_ref[atom * NB + d][:, :COLS])
        mixed = jnp.dot(
            jnp.concatenate(bands, axis=0), near[place], preferred_element_type=jnp.float32
        ).astype(jnp.bfloat16)
        for d, offset in enumerate(OFFSETS):
            blend[(place - offset + REACH) * NB + d] = mixed[64 * d : 64 * (d + 1)]
        return carry

    lax.fori_loop(0, WIDE_BLOCK, blend_from, 0, unroll=2)

    def one_atom(atom):
        total = jnp.zeros((64, 256), jnp.float32)
        for d in range(NB):
            pair = atom * NB + d
            factors = factors_ref[pl.ds(pl.multiple_of(pair * 16, 16), 16), :]
            each, whole = factors[:, :256], factors[:, 256:]
            kron = jnp.concatenate(
                [(each[i : i + 1, :] * whole).astype(jnp.bfloat16) for i in range(NO)], axis=0
            )
            total = total + jnp.dot(
                blend[pair + 2 * REACH * NB], kron, preferred_element_type=jnp.float32
            )
        for x in range(NX):
            for b in range(2):
                row = x * 16 + b * 8
                at = (x * 16 + b) * OUT_STRIDE + atom
                for half in range(2):
                    sums[half, pl.ds(at, NM, stride=2 * OUT_STRIDE), :] = total[
                        row : row + NM, half * 128 : (half + 1) * 128
                    ]

    def some_atoms(step, carry):
        for i in range(UNROLL):
            one_atom(step * UNROLL + i)
        return carry

    lax.fori_loop(0, BLOCK // UNROLL, some_atoms, 0)

    def narrow(i, carry):
        for b in range(2):
            at = pl.multiple_of((2 * i + b) * OUT_STRIDE, 2)
            rows = [sums[half, pl.ds(at, BLOCK), :] for half in range(2)]
            out_ref[i, b * BLOCK : (b + 1) * BLOCK, :] = jnp.concatenate(rows, axis=1).astype(
                jnp.bfloat16
            )
        return carry

    lax.fori_loop(0, NX * NM, narrow, 0, unroll=4)


def self_energy_of(below, own, above, weights, factors):
    vmem = pl.BlockSpec(memory_space=pltpu.VMEM)
    flops = 2 * BLOCK * NB * 64 * (COLS + 256) * 256
    return pl.pallas_call(
        atoms_kernel,
        out_shape=jax.ShapeDtypeStruct((NX * NM, 2 * BLOCK, 256), jnp.bfloat16),
        in_specs=[vmem] * 5,
        out_specs=vmem,
        scratch_shapes=[
            pltpu.VMEM((2, 80 * IN_STRIDE, 128), jnp.float32),
            pltpu.VMEM((WIDE_BLOCK, COLS, 256), jnp.bfloat16),
            pltpu.VMEM(((BLOCK + 4 * REACH) * NB, 64, 256), jnp.bfloat16),
            pltpu.VMEM((2, 64 * OUT_STRIDE, 128), jnp.float32),
        ],
        cost_estimate=pl.CostEstimate(flops=flops, bytes_accessed=16 << 20, transcendentals=0),
        compiler_params=pltpu.CompilerParams(vmem_limit_bytes=20 << 20),
    )(below, own, above, weights, factors)


def body(green_blocks, neighbours, counts, couplings, grad_h, momentum_table):
    packed = packed_blocks(green_blocks.reshape(2, 1024, 256))
    packed, neighbours, counts, couplings, grad_h = lax.optimization_barrier(
        (packed, neighbours, counts, couplings, grad_h)
    )
    own = group_exchange(packed)
    up = [(i, i + 1) for i in range(NZ - 1)]
    below = lax.ppermute(own[NM:], "z", up)
    above = lax.ppermute(own[:-NM], "z", [(b, a) for a, b in up])

    held = atom_data(neighbours, counts, couplings, grad_h)
    choice = column_choice(momentum_table)
    held, own, choice = lax.optimization_barrier((held, own, choice))
    data = group_data(held)
    weights, factors = weights_and_factors(data, choice)
    result = self_energy_of(below, own, above, weights, factors)
    back = group_exchange(result)
    back = back.reshape(NX, NM, 2, BLOCK, 256).transpose(2, 1, 0, 3, 4)
    return back.reshape(2, 1, 1024, 256)


def solution(mesh):
    cube = Mesh(mesh.devices.reshape(NZ, NX, NM), ("z", "x", "m"))
    flat = ("z", "x", "m")
    in_specs = (
        P(("z", "x"), "m", None, None),
        P(flat, None),
        P(flat),
        P(flat, None, None, None),
        P(flat, None, None, None),
        P(),
    )
    out_specs = P(("z", "x"), "m", None, None)
    return jax.shard_map(body, mesh=cube, in_specs=in_specs, out_specs=out_specs, check_vma=False)
```

time: 98.7 us -> 117 us (1.19)
  waiting for transfers between devices: 15.5 us -> 41.8 us
  starting transfers between devices: 30.8 us -> 23.7 us
  blocking collectives: 24.8 us -> 31.9 us
  other arithmetic: 5.03 us -> 0.5 us
  matrix products: 3.66 us -> 0 us
  Pallas kernels: 12.6 us -> 14.3 us
  local copies, waits for them, and re-layouts: 5.68 us -> 4.16 us
    ppermute x3, waiting for transfers between devices: 2.01 us -> 24 us  [atom_data(): held = jnp.concatenate([held, lax.ppermute(held, 'z', pairs)], axis=0)]
    all_to_all x1, waiting for transfers between devices: 1.16 us -> 17.8 us  [group_exchange(): lax.all_to_all(blocks, ('x', 'm'), split_axis=0, concat_axis=0, tiled=True)]
    ppermute x1, waiting for transfers between devices: 11.4 us -> 0.01 us  [body(): above = lax.ppermute(own[:-NM], 'z', [(b, a) for a, b in up])]
    all_to_all x0 -> x1, blocking collectives: none -> 11.2 us  [group_data(): lax.all_to_all(sorted_pieces(held), 'm', split_axis=0, concat_axis=0, til...]
    all_to_all x1 -> x0, starting transfers between devices: 6.04 us -> none  [group_data(): mine = lax.all_to_all(held, 'm', split_axis=0, concat_axis=0, tiled=True)]
    all_to_all x1, blocking collectives: 24.8 us -> 20.7 us  [group_exchange(): lax.all_to_all(blocks, ('x', 'm'), split_axis=0, concat_axis=0, tiled=True)]
    dot_general x3 -> x0, matrix products: 3.66 us -> none  [the longest x1 2.63 us: banded_weights(): jnp.dot(spread, chosen.astype(jnp.bfloat16), preferred_element_type=jnp.b...]
    pallas_call x0 -> x3, Pallas kernels: none -> 3.16 us  [the longest x1 2.33 us: weights_and_factors(): pl.pallas_call(weights_kernel, out_shape=[jax.ShapeDtypeStruct((BLOCK * N...]
  transfers between devices with their start and end apart: 7 -> 6, of which waited for: 6 -> 4; matrix products, arithmetic and copies ran while one was open for 11% -> 1% of each run, Pallas kernels for 0% -> 3%
where the time goes in v3:
time: 117 us
  waiting for transfers between devices  41.8 us (36%)
  blocking collectives  31.9 us (27%)
  starting transfers between devices  23.7 us (20%)
  Pallas kernels  14.3 us (12%)
  local copies, waits for them, and re-layouts  4.16 us (4%)
    ppermute x3, waiting for transfers between devices, atom_data(): held = jnp.concatenate([held, lax.ppermute(held, 'z', pairs)], axis=0)  24 us
    all_to_all x1, blocking collectives, group_exchange(): lax.all_to_all(blocks, ('x', 'm'), split_axis=0, concat_axis=0, tiled=True)  20.7 us
    all_to_all x1, waiting for transfers between devices, group_exchange(): lax.all_to_all(blocks, ('x', 'm'), split_axis=0, concat_axis=0, tiled=True)  17.8 us
    all_to_all x1, blocking collectives, group_data(): lax.all_to_all(sorted_pieces(held), 'm', split_axis=0, concat_axis=0, til...  11.2 us
    ppermute x3, starting transfers between devices, atom_data(): held = jnp.concatenate([held, lax.ppermute(held, 'z', pairs)], axis=0)  10.1 us
    pallas_call x1, Pallas kernels, self_energy_of(): pl.pallas_call(atoms_kernel, out_shape=jax.ShapeDtypeStruct((NX * NM, 2 *...  10 us
    all_to_all x1, starting transfers between devices, group_exchange(): lax.all_to_all(blocks, ('x', 'm'), split_axis=0, concat_axis=0, tiled=True)  8.71 us
    ppermute x1, starting transfers between devices, body(): below = lax.ppermute(own[NM:], 'z', up)  3.58 us
  transfers between devices with their start and end apart: 6, of which 4 were waited for; matrix products, arithmetic and copies ran while one was open for 1% of the time, Pallas kernels for 3%

profile of v3, /device:TPU:1, one launch (start us, length us, event | category | flops | bytes accessed | tf_op | source)
XLA Modules:
  0.0 116.6 jit_solution(11996937052600292058)
XLA Ops:
  0.0 1.2 %copy-done = bf16[2,1,1024,256]{3,2,1,0:T(8,128)(2,1)S(1)} copy-done((bf16[2,1,1024,256]{3,2,1,0:T(8,128)(2,1)S(1)}, bf16[2,1,1024,256]{3,2,1,0:T(8,128)(2,1)}, u32[]{:S(2)}) %copy-start) | copy-done | bytes 1048600
  1.2 1.2 shard_map.64
  2.4 8.7 %all-to-all-start = ((bf16[32,72,256]{2,1,0:T(8,128)(2,1)}), bf16[32,72,256]{2,1,0:T(8,128)(2,1)S(1)}, u32[]{:S(2)}, u32[]{:S(2)}) async-start(bf16[32,72,256]{2,1,0:T(8,128)(2,1)} %shard_map.64), calls=%async_computation | async-start | bytes 2359296 | tf_op jit(solution)/shard_map/all_to_all | solution.py:26
  11.1 0.0 copy-done.2
  11.2 0.1 subtract_select_fusion
  11.3 0.1 broadcast_compare_fusion
  11.3 0.1 select_reduce_fusion
  11.5 0.1 convert_element_type.23
  11.6 0.0 copy-start.1
  11.6 17.8 %all-to-all-done.own_ref = bf16[32,72,256]{2,1,0:T(8,128)(2,1)S(1)} async-done(((bf16[32,72,256]{2,1,0:T(8,128)(2,1)}), bf16[32,72,256]{2,1,0:T(8,128)(2,1)S(1)}, u32[]{:S(2)}, u32[]{:S(2)}) %all-to-all-start) | async-done | bytes 1179680 | tf_op jit(solution)/shard_map/all_to_all | solution.py:26
  29.5 1.3 %fusion = (bf16[24,72,256]{2,1,0:T(8,128)(2,1)}, bf16[24,72,256]{2,1,0:T(8,128)(2,1)}) fusion(bf16[32,72,256]{2,1,0:T(8,128)(2,1)S(1)} %all-to-all-done.own_ref), kind=kLoop, calls=%fused_computation.13 | loop fusion | bytes 3538944 | tf_op jit(solution)/shard_map/slice | solution.py:300
  30.8 3.6 %collective-permute-start = (bf16[24,72,256]{2,1,0:T(8,128)(2,1)}, bf16[24,72,256]{2,1,0:T(8,128)(2,1)S(1)}, u32[]{:S(2)}, u32[]{:S(2)}) collective-permute-start(bf16[24,72,256]{2,1,0:T(8,128)(2,1)} %get-tuple-element.26), channel_id=1, source_target_pairs={{0,32},{32,64},{64,96},{96,128},{128,160},{160,192},{192,224},{1,3... | collective-permute-start | bytes 2654216 | tf_op jit(solution)/shard_map/ppermute | solution.py:299
  34.4 1.3 %collective-permute-start.4 = (bf16[24,72,256]{2,1,0:T(8,128)(2,1)}, bf16[24,72,256]{2,1,0:T(8,128)(2,1)S(1)}, u32[]{:S(2)}, u32[]{:S(2)}) collective-permute-start(bf16[24,72,256]{2,1,0:T(8,128)(2,1)} %get-tuple-element.25), channel_id=1, source_target_pairs={{32,0},{64,32},{96,64},{128,96},{160,128},{192,160},{224,192},{33,... | collective-permute-start | bytes 2654216 | tf_op jit(solution)/shard_map/ppermute | solution.py:300
  35.7 0.0 copy-done.3
  35.7 0.1 select_reduce_fusion.1
  35.9 0.2 copy.11
  36.0 0.1 convert_element_type.25
  36.2 0.1 tile.9
  36.3 2.3 %collective-permute-start.1 = (bf16[1,16,512]{2,1,0:T(8,128)(2,1)S(1)}, bf16[1,16,512]{2,1,0:T(8,128)(2,1)S(1)}, u32[]{:S(2)}, u32[]{:S(2)}) collective-permute-start(bf16[1,16,512]{2,1,0:T(8,128)(2,1)S(1)} %maximum_bitcast_fusion), channel_id=1, source_target_pairs={{0,32},{32,0},{64,96},{96,64},{128,160},{160,128},{192,224},{224,1... | collective-permute-start | bytes 49160 | tf_op jit(solution)/shard_map/ppermute | solution.py:76
  38.6 19.4 %collective-permute-done.1 = bf16[1,16,512]{2,1,0:T(8,128)(2,1)S(1)} collective-permute-done((bf16[1,16,512]{2,1,0:T(8,128)(2,1)S(1)}, bf16[1,16,512]{2,1,0:T(8,128)(2,1)S(1)}, u32[]{:S(2)}, u32[]{:S(2)}) %collective-permute-start.1) | collective-permute-done | bytes 16416 | tf_op jit(solution)/shard_map/ppermute | solution.py:76
  57.9 4.3 %collective-permute-start.2 = (bf16[2,16,512]{2,1,0:T(8,128)(2,1)S(1)}, bf16[2,16,512]{2,1,0:T(8,128)(2,1)S(1)}, u32[]{:S(2)}, u32[]{:S(2)}) collective-permute-start(bf16[2,16,512]{2,1,0:T(8,128)(2,1)S(1)} %pad_maximum_fusion.2), channel_id=1, source_target_pairs={{0,64},{32,96},{64,0},{96,32},{128,192},{160,224},{192,128},{224,1... | collective-permute-start | bytes 98312 | tf_op jit(solution)/shard_map/ppermute | solution.py:76
  62.3 1.7 %collective-permute-done.2 = bf16[2,16,512]{2,1,0:T(8,128)(2,1)S(1)} collective-permute-done((bf16[2,16,512]{2,1,0:T(8,128)(2,1)S(1)}, bf16[2,16,512]{2,1,0:T(8,128)(2,1)S(1)}, u32[]{:S(2)}, u32[]{:S(2)}) %collective-permute-start.2) | collective-permute-done | bytes 32800 | tf_op jit(solution)/shard_map/ppermute | solution.py:76
  64.0 3.4 %collective-permute-start.3 = (bf16[4,16,512]{2,1,0:T(8,128)(2,1)S(1)}, bf16[4,16,512]{2,1,0:T(8,128)(2,1)S(1)}, u32[]{:S(2)}, u32[]{:S(2)}) collective-permute-start(bf16[4,16,512]{2,1,0:T(8,128)(2,1)S(1)} %pad_maximum_fusion.1), channel_id=1, source_target_pairs={{0,128},{32,160},{64,192},{96,224},{128,0},{160,32},{192,64},{224,... | collective-permute-start | bytes 196616 | tf_op jit(solution)/shard_map/ppermute | solution.py:76
  67.4 0.8 shard_map.65.choice_ref
  68.2 3.0 %collective-permute-done.3 = bf16[4,16,512]{2,1,0:T(8,128)(2,1)S(1)} collective-permute-done((bf16[4,16,512]{2,1,0:T(8,128)(2,1)S(1)}, bf16[4,16,512]{2,1,0:T(8,128)(2,1)S(1)}, u32[]{:S(2)}, u32[]{:S(2)}) %collective-permute-start.3) | collective-permute-done | bytes 65568 | tf_op jit(solution)/shard_map/ppermute | solution.py:76
  71.2 11.2 %all_to_all.15 = bf16[8,16,512]{2,1,0:T(8,128)(2,1)S(1)} all-to-all(bf16[8,16,512]{2,1,0:T(8,128)(2,1)S(1)} %shard_map.66), channel_id=1, replica_groups=mesh['z'=8,'x'=4,'m'=8] {'m'}, dimensions={0} | all-to-all | bytes 262144 | tf_op jit(solution)/shard_map/all_to_all | solution.py:99
  82.4 2.3 %shard_map.67 = (bf16[128,64,256]{2,1,0:T(8,128)(2,1)S(1)}, f32[2048,512]{1,0:T(8,128)S(1)}) custom-call(bf16[128,512]{1,0:T(8,128)(2,1)S(1)} %bitcast.13, bf16[256,2048]{1,0:T(8,128)(2,1)S(1)} %shard_map.65.choice_ref), custom_call_target="tpu_custom_call" | custom-call | flops 1073741824 | bytes 6291456 | tf_op jit(solution)/shard_map/pallas_call | solution.py:174
  84.7 0.0 collective-permute-done.below_ref
  84.7 0.0 collective-permute-done.4.above_ref
  84.7 10.0 %shard_map.68 = bf16[32,64,256]{2,1,0:T(8,128)(2,1)S(1)} custom-call(bf16[24,72,256]{2,1,0:T(8,128)(2,1)S(1)} %collective-permute-done.below_ref, bf16[32,72,256]{2,1,0:T(8,128)(2,1)S(1)} %all-to-all-done.own_ref, bf16[24,72,256]{2,1,0:T(8,128)(2,1)S(1)} %collective-permute-done.4.above_ref, bf16[128,64,256]{2,1,0:T(8,128)(2,1)S(1)} %get-tuple-element.23.weights_ref, ...), custom_call_target="tpu_custom_call" | custom-call | flops 1744830464 | bytes 16777216 | tf_op jit(solution)/shard_map/pallas_call | solution.py:276
  94.8 20.7 %all_to_all.16 = bf16[32,64,256]{2,1,0:T(8,128)(2,1)S(1)} all-to-all(bf16[32,64,256]{2,1,0:T(8,128)(2,1)S(1)} %shard_map.68), channel_id=1, replica_groups=mesh['z'=8,'x'=4,'m'=8] {'x','m'}, dimensions={0} | all-to-all | bytes 2097152 | tf_op jit(solution)/shard_map/all_to_all | solution.py:26
  115.5 1.1 copy.12
  (17 shorter events, 0.1 us)
Async XLA Ops:
  0.0 1.2 %copy-start = (bf16[2,1,1024,256]{3,2,1,0:T(8,128)(2,1)S(1)}, bf16[2,1,1024,256]{3,2,1,0:T(8,128)(2,1)}, u32[]{:S(2)}) copy-start(bf16[2,1,1024,256]{3,2,1,0:T(8,128)(2,1)} %param.6) | copy-start | bytes 3145732
  2.4 8.7 %copy-start.2 = (bf16[4,4,16,16]{3,2,1,0:T(8,128)(2,1)S(1)}, bf16[4,4,16,16]{3,2,1,0:T(8,128)(2,1)}, u32[]{:S(2)}) copy-start(bf16[4,4,16,16]{3,2,1,0:T(8,128)(2,1)} %param.10) | copy-start | bytes 24580
  2.4 8.8 %copy-start.4 = (s32[4,4]{1,0:T(4,128)S(1)}, s32[4,4]{1,0:T(4,128)}, u32[]{:S(2)}) copy-start(s32[4,4]{1,0:T(4,128)} %param.7) | copy-start | bytes 196
  2.4 8.8 %copy-start.5 = (s32[4]{0:T(128)S(1)}, s32[4]{0:T(128)}, u32[]{:S(2)}) copy-start(s32[4]{0:T(128)} %param.8) | copy-start | bytes 52
  2.4 27.1 %all-to-all-start = ((bf16[32,72,256]{2,1,0:T(8,128)(2,1)}), bf16[32,72,256]{2,1,0:T(8,128)(2,1)S(1)}, u32[]{:S(2)}, u32[]{:S(2)}) async-start(bf16[32,72,256]{2,1,0:T(8,128)(2,1)} %shard_map.64), calls=%async_computation | async-start | bytes 2359296 | tf_op jit(solution)/shard_map/all_to_all | solution.py:26
  11.6 24.1 %copy-start.3 = (f32[4,4,8,4]{2,3,1,0:T(4,128)S(1)}, f32[4,4,8,4]{2,3,1,0:T(4,128)}, u32[]{:S(2)}) copy-start(f32[4,4,8,4]{2,3,1,0:T(4,128)} %param.9) | copy-start | bytes 6148
  11.6 55.8 %copy-start.1 = (s32[8,8]{1,0:T(8,128)S(1)}, s32[8,8]{1,0:T(8,128)}, u32[]{:S(2)}) copy-start(s32[8,8]{1,0:T(8,128)} %table_ref.1) | copy-start | bytes 772
  30.8 53.9 %collective-permute-start = (bf16[24,72,256]{2,1,0:T(8,128)(2,1)}, bf16[24,72,256]{2,1,0:T(8,128)(2,1)S(1)}, u32[]{:S(2)}, u32[]{:S(2)}) collective-permute-start(bf16[24,72,256]{2,1,0:T(8,128)(2,1)} %get-tuple-element.26), channel_id=1, source_target_pairs={{0,32},{32,64},{64,96},{96,128},{128,160},{160,192},{192,224},{1,3... | collective-permute-start | bytes 2654216 | tf_op jit(solution)/shard_map/ppermute | solution.py:299
  34.4 50.3 %collective-permute-start.4 = (bf16[24,72,256]{2,1,0:T(8,128)(2,1)}, bf16[24,72,256]{2,1,0:T(8,128)(2,1)S(1)}, u32[]{:S(2)}, u32[]{:S(2)}) collective-permute-start(bf16[24,72,256]{2,1,0:T(8,128)(2,1)} %get-tuple-element.25), channel_id=1, source_target_pairs={{32,0},{64,32},{96,64},{128,96},{160,128},{192,160},{224,192},{33,... | collective-permute-start | bytes 2654216 | tf_op jit(solution)/shard_map/ppermute | solution.py:300
  36.3 21.7 %collective-permute-start.1 = (bf16[1,16,512]{2,1,0:T(8,128)(2,1)S(1)}, bf16[1,16,512]{2,1,0:T(8,128)(2,1)S(1)}, u32[]{:S(2)}, u32[]{:S(2)}) collective-permute-start(bf16[1,16,512]{2,1,0:T(8,128)(2,1)S(1)} %maximum_bitcast_fusion), channel_id=1, source_target_pairs={{0,32},{32,0},{64,96},{96,64},{128,160},{160,128},{192,224},{224,1... | collective-permute-start | bytes 49160 | tf_op jit(solution)/shard_map/ppermute | solution.py:76
  57.9 6.0 %collective-permute-start.2 = (bf16[2,16,512]{2,1,0:T(8,128)(2,1)S(1)}, bf16[2,16,512]{2,1,0:T(8,128)(2,1)S(1)}, u32[]{:S(2)}, u32[]{:S(2)}) collective-permute-start(bf16[2,16,512]{2,1,0:T(8,128)(2,1)S(1)} %pad_maximum_fusion.2), channel_id=1, source_target_pairs={{0,64},{32,96},{64,0},{96,32},{128,192},{160,224},{192,128},{224,1... | collective-permute-start | bytes 98312 | tf_op jit(solution)/shard_map/ppermute | solution.py:76
  64.0 7.2 %collective-permute-start.3 = (bf16[4,16,512]{2,1,0:T(8,128)(2,1)S(1)}, bf16[4,16,512]{2,1,0:T(8,128)(2,1)S(1)}, u32[]{:S(2)}, u32[]{:S(2)}) collective-permute-start(bf16[4,16,512]{2,1,0:T(8,128)(2,1)S(1)} %pad_maximum_fusion.1), channel_id=1, source_target_pairs={{0,128},{32,160},{64,192},{96,224},{128,0},{160,32},{192,64},{224,... | collective-permute-start | bytes 196616 | tf_op jit(solution)/shard_map/ppermute | solution.py:76

commit v4 on v3

--- a/solution.py
+++ b/solution.py
@@ -1,3 +1,5 @@
+import functools
+
 import jax
 import jax.numpy as jnp
 from jax import lax
@@ -17,7 +19,9 @@
 WIDE_BLOCK = BLOCK + 2 * REACH
 COLS = 160
 UNROLL = 2
-IN_STRIDE, OUT_STRIDE = 76, 34
+FIRST = 24
+EARLY = FIRST + 2 * REACH
+LATE = WIDE_BLOCK - EARLY
 OFFSETS = (-2, -1, 1, 2)
 CHUNK = 32
 
@@ -26,32 +30,52 @@
     return lax.all_to_all(blocks, ("x", "m"), split_axis=0, concat_axis=0, tiled=True)
 
 
-def pack_kernel(green_ref, out_ref):
+def pack_kernel(green_ref, out_ref, taken, made, in_sems, out_sems):
+    loads = []
     for m in range(NM):
+        rows = pl.ds(m * NX * BLOCK, NX * BLOCK)
+        copy = pltpu.make_async_copy(green_ref.at[:, rows], taken.at[:, rows], in_sems.at[m])
+        copy.start()
+        loads.append(copy)
+    loads[0].wait()
+    stores = []
+    for m in range(NM):
+        if m + 1 < NM:
+            loads[m + 1].wait()
         for x in range(NX):
             first = (m * NX + x) * BLOCK
+            before, after = max(first - 16, 0), min(first + BLOCK, 1024 - 16)
+            early, late = [], []
+            for b in range(2):
+                left = taken[b, before : before + 16, :][16 - REACH :]
+                right = taken[b, after : after + 16, :][:REACH]
+                whole = jnp.concatenate([left, taken[b, first : first + BLOCK, :], right], axis=0)
+                early.append(whole[:EARLY])
+                late.append(whole[EARLY:])
             dest = x * NM + m
-            halo = []
-            for b in range(2):
-                out_ref[dest, b * BLOCK : (b + 1) * BLOCK, :] = green_ref[
-                    b, first : first + BLOCK, :
-                ]
-                left = green_ref[b, max(first - 16, 0) : max(first - 16, 0) + 16, :][16 - REACH :]
-                after = min(first + BLOCK, 1024 - 16)
-                right = green_ref[b, after : after + 16, :][:REACH]
-                halo += [left, right]
-            out_ref[dest, 2 * BLOCK :, :] = jnp.concatenate(halo, axis=0)
+            made[dest] = jnp.concatenate(early + late, axis=0)
+            copy = pltpu.make_async_copy(made.at[dest], out_ref.at[dest], out_sems.at[dest])
+            copy.start()
+            stores.append(copy)
+    for copy in stores:
+        copy.wait()
 
 
 def packed_blocks(green):
-    vmem = pl.BlockSpec(memory_space=pltpu.VMEM)
+    shape = (NX * NM, 2 * WIDE_BLOCK, 256)
     return pl.pallas_call(
         pack_kernel,
-        out_shape=jax.ShapeDtypeStruct((NX * NM, 2 * WIDE_BLOCK, 256), green.dtype),
-        in_specs=[vmem],
-        out_specs=vmem,
+        out_shape=jax.ShapeDtypeStruct(shape, green.dtype),
+        in_specs=[pl.BlockSpec(memory_space=pltpu.HBM)],
+        out_specs=pl.BlockSpec(memory_space=pltpu.HBM),
+        scratch_shapes=[
+            pltpu.VMEM(green.shape, green.dtype),
+            pltpu.VMEM(shape, green.dtype),
+            pltpu.SemaphoreType.DMA((NM,)),
+            pltpu.SemaphoreType.DMA((NX * NM,)),
+        ],
         cost_estimate=pl.CostEstimate(flops=1 << 22, bytes_accessed=2 << 20, transcendentals=0),
-        compiler_params=pltpu.CompilerParams(vmem_limit_bytes=8 << 20),
+        compiler_params=pltpu.CompilerParams(vmem_limit_bytes=62 << 20),
     )(green)
 
 
@@ -184,42 +208,51 @@
     )(data, choice)
 
 
-def atoms_kernel(
-    below_ref, own_ref, above_ref, weights_ref, factors_ref, out_ref, lanes, near, blend, sums
-):
+def atoms_kernel(begin, end, *refs):
+    count = end - begin
+    early = begin == 0
+    if early:
+        below_ref, own_ref, above_ref, weights_ref, factors_ref, out_ref, edge_ref = refs[:7]
+        width, skip, known = EARLY, 0, 0
+    else:
+        below_ref, own_ref, above_ref, weights_ref, factors_ref, edge_ref, ready_ref, out_ref = refs[:8]
+        width, skip, known = LATE, 2 * EARLY, 2 * REACH
+    lanes, near, blend, sums = refs[-4:]
+    stride, out_stride = 2 * width + 4, count + 2
+
     done = 0
     for part in (below_ref, own_ref, above_ref):
-
-        def widen(i, carry, part=part, done=done):
-            rows = part[i].astype(jnp.float32)
-            at = pl.multiple_of((done + i) * IN_STRIDE, 4)
+        at_row = skip if part is own_ref else 0
+
+        def widen(i, carry, part=part, done=done, at_row=at_row):
+            rows = part[i, at_row : at_row + 2 * width].astype(jnp.float32)
+            at = pl.multiple_of((done + i) * stride, 4)
             for half in range(2):
-                lanes[half, pl.ds(at, 72), :] = rows[:, half * 128 : (half + 1) * 128]
+                lanes[half, pl.ds(at, 2 * width), :] = rows[:, half * 128 : (half + 1) * 128]
             return carry
 
         lax.fori_loop(0, part.shape[0], widen, 0, unroll=4)
         done += part.shape[0]
 
-    def regroup(place, start, step):
+    def regroup(place, carry):
         for b in range(2):
             for half in range(2):
-                rows = lanes[half, pl.ds(start + b * step, 80, stride=IN_STRIDE), :]
-                near[place, b * 80 : (b + 1) * 80, half * 128 : (half + 1) * 128] = rows.astype(
-                    jnp.bfloat16
+                rows = lanes[half, pl.ds(place + b * width, 80, stride=stride), :]
+                near[known + place, b * 80 : (b + 1) * 80, half * 128 : (half + 1) * 128] = (
+                    rows.astype(jnp.bfloat16)
                 )
-
-    def regroup_atom(atom, carry):
-        regroup(REACH + atom, atom, BLOCK)
-        return carry
-
-    lax.fori_loop(0, BLOCK, regroup_atom, 0, unroll=2)
-    for h in range(2 * REACH):
-        regroup(h if h < REACH else BLOCK + h, 2 * BLOCK + h, 2 * REACH)
+        return carry
+
+    lax.fori_loop(0, width, regroup, 0, unroll=2)
+    if early:
+        edge_ref[...] = near[count:]
+    else:
+        near[:known] = edge_ref[...]
 
     def blend_from(place, carry):
         bands = []
         for d, offset in enumerate(OFFSETS):
-            atom = jnp.clip(place - REACH - offset, 0, BLOCK - 1)
+            atom = jnp.clip(begin + place - REACH - offset, 0, BLOCK - 1)
             bands.append(weights_ref[atom * NB + d][:, :COLS])
         mixed = jnp.dot(
             jnp.concatenate(bands, axis=0), near[place], preferred_element_type=jnp.float32
@@ -228,26 +261,26 @@
             blend[(place - offset + REACH) * NB + d] = mixed[64 * d : 64 * (d + 1)]
         return carry
 
-    lax.fori_loop(0, WIDE_BLOCK, blend_from, 0, unroll=2)
+    lax.fori_loop(0, count + 2 * REACH, blend_from, 0, unroll=2)
 
     def one_atom(atom):
         total = jnp.zeros((64, 256), jnp.float32)
         for d in range(NB):
-            pair = atom * NB + d
-            factors = factors_ref[pl.ds(pl.multiple_of(pair * 16, 16), 16), :]
+            row = pl.multiple_of(((begin + atom) * NB + d) * NO, NO)
+            factors = factors_ref[pl.ds(row, NO), :]
             each, whole = factors[:, :256], factors[:, 256:]
             kron = jnp.concatenate(
                 [(each[i : i + 1, :] * whole).astype(jnp.bfloat16) for i in range(NO)], axis=0
             )
             total = total + jnp.dot(
-                blend[pair + 2 * REACH * NB], kron, preferred_element_type=jnp.float32
+                blend[(atom + 2 * REACH) * NB + d], kron, preferred_element_type=jnp.float32
             )
         for x in range(NX):
             for b in range(2):
                 row = x * 16 + b * 8
-                at = (x * 16 + b) * OUT_STRIDE + atom
+                at = (x * 16 + b) * out_stride + atom
                 for half in range(2):
-                    sums[half, pl.ds(at, NM, stride=2 * OUT_STRIDE), :] = total[
+                    sums[half, pl.ds(at, NM, stride=2 * out_stride), :] = total[
                         row : row + NM, half * 128 : (half + 1) * 128
                     ]
 
@@ -256,37 +289,43 @@
             one_atom(step * UNROLL + i)
         return carry
 
-    lax.fori_loop(0, BLOCK // UNROLL, some_atoms, 0)
+    lax.fori_loop(0, count // UNROLL, some_atoms, 0)
 
     def narrow(i, carry):
         for b in range(2):
-            at = pl.multiple_of((2 * i + b) * OUT_STRIDE, 2)
-            rows = [sums[half, pl.ds(at, BLOCK), :] for half in range(2)]
-            out_ref[i, b * BLOCK : (b + 1) * BLOCK, :] = jnp.concatenate(rows, axis=1).astype(
-                jnp.bfloat16
-            )
+            at = pl.multiple_of((2 * i + b) * out_stride, 2)
+            rows = [sums[half, pl.ds(at, count), :] for half in range(2)]
+            rows = jnp.concatenate(rows, axis=1)
+            if not early:
+                before = ready_ref[i, b * BLOCK : (b + 1) * BLOCK, :].astype(jnp.float32)
+                rows = jnp.concatenate([before[:begin], rows], axis=0)
+            out_ref[i, b * BLOCK : b * BLOCK + end, :] = rows.astype(jnp.bfloat16)
         return carry
 
     lax.fori_loop(0, NX * NM, narrow, 0, unroll=4)
 
 
-def self_energy_of(below, own, above, weights, factors):
+def self_energy_of(begin, end, *operands):
     vmem = pl.BlockSpec(memory_space=pltpu.VMEM)
-    flops = 2 * BLOCK * NB * 64 * (COLS + 256) * 256
-    return pl.pallas_call(
-        atoms_kernel,
-        out_shape=jax.ShapeDtypeStruct((NX * NM, 2 * BLOCK, 256), jnp.bfloat16),
-        in_specs=[vmem] * 5,
-        out_specs=vmem,
+    count = end - begin
+    width = EARLY if begin == 0 else LATE
+    flops = 2 * count * NB * 64 * (COLS + 256) * 256
+    out = jax.ShapeDtypeStruct((NX * NM, 2 * BLOCK, 256), jnp.bfloat16)
+    edge = jax.ShapeDtypeStruct((2 * REACH, COLS, 256), jnp.bfloat16)
+    return pl.pallas_call(
+        functools.partial(atoms_kernel, begin, end),
+        out_shape=[out, edge] if begin == 0 else out,
+        in_specs=[vmem] * len(operands),
+        out_specs=[vmem, vmem] if begin == 0 else vmem,
         scratch_shapes=[
-            pltpu.VMEM((2, 80 * IN_STRIDE, 128), jnp.float32),
-            pltpu.VMEM((WIDE_BLOCK, COLS, 256), jnp.bfloat16),
-            pltpu.VMEM(((BLOCK + 4 * REACH) * NB, 64, 256), jnp.bfloat16),
-            pltpu.VMEM((2, 64 * OUT_STRIDE, 128), jnp.float32),
+            pltpu.VMEM((2, 80 * (2 * width + 4), 128), jnp.float32),
+            pltpu.VMEM((count + 2 * REACH, COLS, 256), jnp.bfloat16),
+            pltpu.VMEM(((count + 4 * REACH) * NB, 64, 256), jnp.bfloat16),
+            pltpu.VMEM((2, 64 * (count + 2), 128), jnp.float32),
         ],
-        cost_estimate=pl.CostEstimate(flops=flops, bytes_accessed=16 << 20, transcendentals=0),
+        cost_estimate=pl.CostEstimate(flops=flops, bytes_accessed=8 << 20, transcendentals=0),
         compiler_params=pltpu.CompilerParams(vmem_limit_bytes=20 << 20),
-    )(below, own, above, weights, factors)
+    )(*operands)
 
 
 def body(green_blocks, neighbours, counts, couplings, grad_h, momentum_table):
@@ -296,15 +335,27 @@
     )
     own = group_exchange(packed)
     up = [(i, i + 1) for i in range(NZ - 1)]
-    below = lax.ppermute(own[NM:], "z", up)
-    above = lax.ppermute(own[:-NM], "z", [(b, a) for a, b in up])
-
+    down = [(b, a) for a, b in up]
+
+    def exchanged(rows):
+        below = lax.ppermute(own[NM:, rows], "z", up)
+        above = lax.ppermute(own[:-NM, rows], "z", down)
+        return below, above
+
+    below, above = exchanged(slice(0, 2 * EARLY))
     held = atom_data(neighbours, counts, couplings, grad_h)
     choice = column_choice(momentum_table)
     held, own, choice = lax.optimization_barrier((held, own, choice))
     data = group_data(held)
+    data, own = lax.optimization_barrier((data, own))
+    late_below, late_above = exchanged(slice(2 * EARLY, 2 * WIDE_BLOCK))
     weights, factors = weights_and_factors(data, choice)
-    result = self_energy_of(below, own, above, weights, factors)
+    result, edge = self_energy_of(
+        0, FIRST, below, own, above, weights, factors
+    )
+    result = self_energy_of(
+        FIRST, BLOCK, late_below, own, late_above, weights, factors, edge, result
+    )
     back = group_exchange(result)
     back = back.reshape(NX, NM, 2, BLOCK, 256).transpose(2, 1, 0, 3, 4)
     return back.reshape(2, 1, 1024, 256)

time: 117 us -> 107 us (0.915)
  waiting for transfers between devices: 41.8 us -> 24.5 us
  starting transfers between devices: 23.7 us -> 33.1 us
  local copies, waits for them, and re-layouts: 4.16 us -> 1.72 us
  Pallas kernels: 14.3 us -> 16.2 us
  blocking collectives: 31.9 us -> 30.6 us
    ppermute x3, waiting for transfers between devices: 24 us -> 13.4 us  [atom_data(): held = jnp.concatenate([held, lax.ppermute(held, 'z', pairs)], axis=0)]
    all_to_all x1, waiting for transfers between devices: 17.8 us -> 11.1 us  [group_exchange(): lax.all_to_all(blocks, ('x', 'm'), split_axis=0, concat_axis=0, tiled=True)]
    ppermute x2 -> x4, starting transfers between devices: 4.88 us -> 10.9 us  [the longest x2 8.34 us: exchanged(): below = lax.ppermute(own[NM:, rows], 'z', up)]
    ppermute x3, starting transfers between devices: 10.1 us -> 13.4 us  [atom_data(): held = jnp.concatenate([held, lax.ppermute(held, 'z', pairs)], axis=0)]
    pallas_call x2 -> x3, Pallas kernels: 11.2 us -> 13 us  [the longest x2 10.6 us: self_energy_of(): pl.pallas_call(functools.partial(atoms_kernel, begin, end), out_shape=[ou...]
    all_to_all x1, blocking collectives: 11.2 us -> 9.32 us  [group_data(): lax.all_to_all(sorted_pieces(held), 'm', split_axis=0, concat_axis=0, til...]
    slice x1 -> x2, local copies, waits for them, and re-layouts: 1.34 us -> 0.12 us  [exchanged(): above = lax.ppermute(own[:-NM, rows], 'z', down)]
    unnamed x12 -> x10, local copies, waits for them, and re-layouts: 1.25 us -> 0.03 us
  transfers between devices with their start and end apart: 6 -> 8, of which waited for: 4 -> 3; matrix products, arithmetic and copies ran while one was open for 1% -> 1% of each run, Pallas kernels for 3% -> 10%
where the time goes in v4:
time: 107 us
  starting transfers between devices  33.1 us (31%)
  blocking collectives  30.6 us (29%)
  waiting for transfers between devices  24.5 us (23%)
  Pallas kernels  16.2 us (15%)
  local copies, waits for them, and re-layouts  1.72 us (2%)
    all_to_all x1, blocking collectives, group_exchange(): lax.all_to_all(blocks, ('x', 'm'), split_axis=0, concat_axis=0, tiled=True)  21.3 us
    ppermute x3, waiting for transfers between devices, atom_data(): held = jnp.concatenate([held, lax.ppermute(held, 'z', pairs)], axis=0)  13.4 us
    ppermute x3, starting transfers between devices, atom_data(): held = jnp.concatenate([held, lax.ppermute(held, 'z', pairs)], axis=0)  13.4 us
    all_to_all x1, waiting for transfers between devices, group_exchange(): lax.all_to_all(blocks, ('x', 'm'), split_axis=0, concat_axis=0, tiled=True)  11.1 us
    pallas_call x2, Pallas kernels, self_energy_of(): pl.pallas_call(functools.partial(atoms_kernel, begin, end), out_shape=[ou...  10.6 us
    all_to_all x1, blocking collectives, group_data(): lax.all_to_all(sorted_pieces(held), 'm', split_axis=0, concat_axis=0, til...  9.32 us
    all_to_all x1, starting transfers between devices, group_exchange(): lax.all_to_all(blocks, ('x', 'm'), split_axis=0, concat_axis=0, tiled=True)  8.72 us
    ppermute x2, starting transfers between devices, exchanged(): below = lax.ppermute(own[NM:, rows], 'z', up)  8.34 us
  transfers between devices with their start and end apart: 8, of which 3 were waited for; matrix products, arithmetic and copies ran while one was open for 1% of the time, Pallas kernels for 10%

profile of v4, /device:TPU:1, one launch (start us, length us, event | category | flops | bytes accessed | tf_op | source)
XLA Modules:
  0.0 106.9 jit_solution(18206676382467833182)
XLA Ops:
  0.0 2.4 %shard_map.64 = bf16[32,72,256]{2,1,0:T(8,128)(2,1)} custom-call(bf16[2,1024,256]{2,1,0:T(8,128)(2,1)} %bitcast.14), custom_call_target="tpu_custom_call" | custom-call | flops 4194304 | bytes 2097152 | tf_op jit(solution)/shard_map/pallas_call | solution.py:66
  2.4 0.0 copy-start.1
  2.4 0.0 copy-start.3
  2.4 0.0 copy-start.4
  2.4 0.0 copy-start.2
  2.4 8.7 %all-to-all-start = ((bf16[32,72,256]{2,1,0:T(8,128)(2,1)}), bf16[32,72,256]{2,1,0:T(8,128)(2,1)S(1)}, u32[]{:S(2)}, u32[]{:S(2)}) async-start(bf16[32,72,256]{2,1,0:T(8,128)(2,1)} %shard_map.64), calls=%async_computation | async-start | bytes 2359296 | tf_op jit(solution)/shard_map/all_to_all | solution.py:30
  11.3 0.1 subtract_select_fusion
  11.3 0.1 broadcast_compare_fusion
  11.4 0.1 select_reduce_fusion
  11.5 0.1 convert_element_type.23
  11.7 0.1 select_reduce_fusion.1
  11.8 0.2 copy.11
  12.0 0.1 convert_element_type.25
  12.1 0.1 tile.9
  12.2 1.7 %collective-permute-start = (bf16[1,16,512]{2,1,0:T(8,128)(2,1)S(1)}, bf16[1,16,512]{2,1,0:T(8,128)(2,1)S(1)}, u32[]{:S(2)}, u32[]{:S(2)}) collective-permute-start(bf16[1,16,512]{2,1,0:T(8,128)(2,1)S(1)} %maximum_bitcast_fusion), channel_id=1, source_target_pairs={{0,32},{32,0},{64,96},{96,64},{128,160},{160,128},{192,224},{224,1... | collective-permute-start | bytes 49160 | tf_op jit(solution)/shard_map/ppermute | solution.py:100
  13.9 1.4 %collective-permute-done = bf16[1,16,512]{2,1,0:T(8,128)(2,1)S(1)} collective-permute-done((bf16[1,16,512]{2,1,0:T(8,128)(2,1)S(1)}, bf16[1,16,512]{2,1,0:T(8,128)(2,1)S(1)}, u32[]{:S(2)}, u32[]{:S(2)}) %collective-permute-start) | collective-permute-done | bytes 16416 | tf_op jit(solution)/shard_map/ppermute | solution.py:100
  15.4 3.1 %collective-permute-start.1 = (bf16[2,16,512]{2,1,0:T(8,128)(2,1)S(1)}, bf16[2,16,512]{2,1,0:T(8,128)(2,1)S(1)}, u32[]{:S(2)}, u32[]{:S(2)}) collective-permute-start(bf16[2,16,512]{2,1,0:T(8,128)(2,1)S(1)} %pad_maximum_fusion.2), channel_id=1, source_target_pairs={{0,64},{32,96},{64,0},{96,32},{128,192},{160,224},{192,128},{224,1... | collective-permute-start | bytes 98312 | tf_op jit(solution)/shard_map/ppermute | solution.py:100
  18.5 11.1 %all-to-all-done.refs_1_ = bf16[32,72,256]{2,1,0:T(8,128)(2,1)S(1)} async-done(((bf16[32,72,256]{2,1,0:T(8,128)(2,1)}), bf16[32,72,256]{2,1,0:T(8,128)(2,1)S(1)}, u32[]{:S(2)}, u32[]{:S(2)}) %all-to-all-start) | async-done | bytes 1179680 | tf_op jit(solution)/shard_map/all_to_all | solution.py:30
  29.5 0.1 fusion
  29.6 3.6 %collective-permute-start.5 = (bf16[24,56,256]{2,1,0:T(8,128)(2,1)S(1)}, bf16[24,56,256]{2,1,0:T(8,128)(2,1)S(1)}, u32[]{:S(2)}, u32[]{:S(2)}) collective-permute-start(bf16[24,56,256]{2,1,0:T(8,128)(2,1)S(1)} %get-tuple-element.34), channel_id=1, source_target_pairs={{0,32},{32,64},{64,96},{96,128},{128,160},{160,192},{192,224},{1,3... | collective-permute-start | bytes 2064392 | tf_op jit(solution)/shard_map/ppermute | solution.py:341
  33.2 1.3 %collective-permute-start.6 = (bf16[24,56,256]{2,1,0:T(8,128)(2,1)S(1)}, bf16[24,56,256]{2,1,0:T(8,128)(2,1)S(1)}, u32[]{:S(2)}, u32[]{:S(2)}) collective-permute-start(bf16[24,56,256]{2,1,0:T(8,128)(2,1)S(1)} %get-tuple-element.33), channel_id=1, source_target_pairs={{32,0},{64,32},{96,64},{128,96},{160,128},{192,160},{224,192},{33,... | collective-permute-start | bytes 2064392 | tf_op jit(solution)/shard_map/ppermute | solution.py:342
  34.5 8.6 %collective-permute-start.2 = (bf16[4,16,512]{2,1,0:T(8,128)(2,1)S(1)}, bf16[4,16,512]{2,1,0:T(8,128)(2,1)S(1)}, u32[]{:S(2)}, u32[]{:S(2)}) collective-permute-start(bf16[4,16,512]{2,1,0:T(8,128)(2,1)S(1)} %pad_maximum_fusion.1), channel_id=1, source_target_pairs={{0,128},{32,160},{64,192},{96,224},{128,0},{160,32},{192,64},{224,... | collective-permute-start | bytes 196616 | tf_op jit(solution)/shard_map/ppermute | solution.py:100
  43.2 0.8 shard_map.65.choice_ref
  44.0 12.0 %collective-permute-done.2 = bf16[4,16,512]{2,1,0:T(8,128)(2,1)S(1)} collective-permute-done((bf16[4,16,512]{2,1,0:T(8,128)(2,1)S(1)}, bf16[4,16,512]{2,1,0:T(8,128)(2,1)S(1)}, u32[]{:S(2)}, u32[]{:S(2)}) %collective-permute-start.2) | collective-permute-done | bytes 65568 | tf_op jit(solution)/shard_map/ppermute | solution.py:100
  56.0 9.3 %all_to_all.15 = bf16[8,16,512]{2,1,0:T(8,128)(2,1)S(1)} all-to-all(bf16[8,16,512]{2,1,0:T(8,128)(2,1)S(1)} %shard_map.66), channel_id=1, replica_groups=mesh['z'=8,'x'=4,'m'=8] {'m'}, dimensions={0} | all-to-all | bytes 262144 | tf_op jit(solution)/shard_map/all_to_all | solution.py:123
  65.4 4.8 %collective-permute-start.3 = (bf16[24,16,256]{2,1,0:T(8,128)(2,1)S(1)}, bf16[24,16,256]{2,1,0:T(8,128)(2,1)S(1)}, u32[]{:S(2)}, u32[]{:S(2)}) collective-permute-start(bf16[24,16,256]{2,1,0:T(8,128)(2,1)S(1)} %get-tuple-element.36), channel_id=1, source_target_pairs={{0,32},{32,64},{64,96},{96,128},{128,160},{160,192},{192,224},{1,3... | collective-permute-start | bytes 589832 | tf_op jit(solution)/shard_map/ppermute | solution.py:341
  70.2 1.3 %collective-permute-start.4 = (bf16[24,16,256]{2,1,0:T(8,128)(2,1)S(1)}, bf16[24,16,256]{2,1,0:T(8,128)(2,1)S(1)}, u32[]{:S(2)}, u32[]{:S(2)}) collective-permute-start(bf16[24,16,256]{2,1,0:T(8,128)(2,1)S(1)} %get-tuple-element.35), channel_id=1, source_target_pairs={{32,0},{64,32},{96,64},{128,96},{160,128},{192,160},{224,192},{33,... | collective-permute-start | bytes 589832 | tf_op jit(solution)/shard_map/ppermute | solution.py:342
  71.5 2.3 %shard_map.67 = (bf16[128,64,256]{2,1,0:T(8,128)(2,1)S(1)}, f32[2048,512]{1,0:T(8,128)S(1)}) custom-call(bf16[128,512]{1,0:T(8,128)(2,1)S(1)} %bitcast.12, bf16[256,2048]{1,0:T(8,128)(2,1)S(1)} %shard_map.65.choice_ref), custom_call_target="tpu_custom_call" | custom-call | flops 1073741824 | bytes 6291456 | tf_op jit(solution)/shard_map/pallas_call | solution.py:198
  73.8 7.7 %shard_map.68 = (bf16[32,64,256]{2,1,0:T(8,128)(2,1)S(1)}, bf16[4,160,256]{2,1,0:T(8,128)(2,1)S(1)}) custom-call(bf16[24,56,256]{2,1,0:T(8,128)(2,1)S(1)} %collective-permute-done.5.refs_0_, bf16[32,72,256]{2,1,0:T(8,128)(2,1)S(1)} %all-to-all-done.refs_1_, bf16[24,56,256]{2,1,0:T(8,128)(2,1)S(1)} %collective-permute-done.6.refs_2_, ...), custom_call_target="tpu_custom_call" | custom-call | flops 1308622848 | bytes 8388608 | tf_op jit(solution)/shard_map/pallas_call | solution.py:315
  81.5 2.9 %shard_map.69 = bf16[32,64,256]{2,1,0:T(8,128)(2,1)S(1)} custom-call(bf16[24,16,256]{2,1,0:T(8,128)(2,1)S(1)} %collective-permute-done.3.refs_0_, bf16[32,72,256]{2,1,0:T(8,128)(2,1)S(1)} %all-to-all-done.refs_1_, bf16[24,16,256]{2,1,0:T(8,128)(2,1)S(1)} %collective-permute-done.4.refs_2_, bf16[128,64,256]{2,1,0:T(8,128)(2,1)S(1)} %get-tuple-element.29.refs_3_, ...), custom_call_target="tpu_custom_call" | custom-call | flops 436207616 | bytes 8388608 | tf_op jit(solution)/shard_map/pallas_call | solution.py:315
  84.5 21.3 %all_to_all.16 = bf16[32,64,256]{2,1,0:T(8,128)(2,1)S(1)} all-to-all(bf16[32,64,256]{2,1,0:T(8,128)(2,1)S(1)} %shard_map.69), channel_id=1, replica_groups=mesh['z'=8,'x'=4,'m'=8] {'x','m'}, dimensions={0} | all-to-all | bytes 2097152 | tf_op jit(solution)/shard_map/all_to_all | solution.py:30
  105.8 1.1 copy.12
  (21 shorter events, 0.1 us)
Async XLA Ops:
  2.4 8.8 %copy-start.1 = (bf16[4,4,16,16]{3,2,1,0:T(8,128)(2,1)S(1)}, bf16[4,4,16,16]{3,2,1,0:T(8,128)(2,1)}, u32[]{:S(2)}) copy-start(bf16[4,4,16,16]{3,2,1,0:T(8,128)(2,1)} %param.10) | copy-start | bytes 24580
  2.4 8.8 %copy-start.3 = (s32[4,4]{1,0:T(4,128)S(1)}, s32[4,4]{1,0:T(4,128)}, u32[]{:S(2)}) copy-start(s32[4,4]{1,0:T(4,128)} %param.7) | copy-start | bytes 196
  2.4 8.8 %copy-start.4 = (s32[4]{0:T(128)S(1)}, s32[4]{0:T(128)}, u32[]{:S(2)}) copy-start(s32[4]{0:T(128)} %param.8) | copy-start | bytes 52
  2.4 9.2 %copy-start.2 = (f32[4,4,8,4]{2,3,1,0:T(4,128)S(1)}, f32[4,4,8,4]{2,3,1,0:T(4,128)}, u32[]{:S(2)}) copy-start(f32[4,4,8,4]{2,3,1,0:T(4,128)} %param.9) | copy-start | bytes 6148
  2.4 27.1 %all-to-all-start = ((bf16[32,72,256]{2,1,0:T(8,128)(2,1)}), bf16[32,72,256]{2,1,0:T(8,128)(2,1)S(1)}, u32[]{:S(2)}, u32[]{:S(2)}) async-start(bf16[32,72,256]{2,1,0:T(8,128)(2,1)} %shard_map.64), calls=%async_computation | async-start | bytes 2359296 | tf_op jit(solution)/shard_map/all_to_all | solution.py:30
  12.2 3.1 %collective-permute-start = (bf16[1,16,512]{2,1,0:T(8,128)(2,1)S(1)}, bf16[1,16,512]{2,1,0:T(8,128)(2,1)S(1)}, u32[]{:S(2)}, u32[]{:S(2)}) collective-permute-start(bf16[1,16,512]{2,1,0:T(8,128)(2,1)S(1)} %maximum_bitcast_fusion), channel_id=1, source_target_pairs={{0,32},{32,0},{64,96},{96,64},{128,160},{160,128},{192,224},{224,1... | collective-permute-start | bytes 49160 | tf_op jit(solution)/shard_map/ppermute | solution.py:100
  15.4 27.8 %copy-start = (s32[8,8]{1,0:T(8,128)S(1)}, s32[8,8]{1,0:T(8,128)}, u32[]{:S(2)}) copy-start(s32[8,8]{1,0:T(8,128)} %table_ref.1) | copy-start | bytes 772
  15.4 19.1 %collective-permute-start.1 = (bf16[2,16,512]{2,1,0:T(8,128)(2,1)S(1)}, bf16[2,16,512]{2,1,0:T(8,128)(2,1)S(1)}, u32[]{:S(2)}, u32[]{:S(2)}) collective-permute-start(bf16[2,16,512]{2,1,0:T(8,128)(2,1)S(1)} %pad_maximum_fusion.2), channel_id=1, source_target_pairs={{0,64},{32,96},{64,0},{96,32},{128,192},{160,224},{192,128},{224,1... | collective-permute-start | bytes 98312 | tf_op jit(solution)/shard_map/ppermute | solution.py:100
  29.6 44.2 %collective-permute-start.5 = (bf16[24,56,256]{2,1,0:T(8,128)(2,1)S(1)}, bf16[24,56,256]{2,1,0:T(8,128)(2,1)S(1)}, u32[]{:S(2)}, u32[]{:S(2)}) collective-permute-start(bf16[24,56,256]{2,1,0:T(8,128)(2,1)S(1)} %get-tuple-element.34), channel_id=1, source_target_pairs={{0,32},{32,64},{64,96},{96,128},{128,160},{160,192},{192,224},{1,3... | collective-permute-start | bytes 2064392 | tf_op jit(solution)/shard_map/ppermute | solution.py:341
  33.2 40.6 %collective-permute-start.6 = (bf16[24,56,256]{2,1,0:T(8,128)(2,1)S(1)}, bf16[24,56,256]{2,1,0:T(8,128)(2,1)S(1)}, u32[]{:S(2)}, u32[]{:S(2)}) collective-permute-start(bf16[24,56,256]{2,1,0:T(8,128)(2,1)S(1)} %get-tuple-element.33), channel_id=1, source_target_pairs={{32,0},{64,32},{96,64},{128,96},{160,128},{192,160},{224,192},{33,... | collective-permute-start | bytes 2064392 | tf_op jit(solution)/shard_map/ppermute | solution.py:342
  34.5 21.4 %collective-permute-start.2 = (bf16[4,16,512]{2,1,0:T(8,128)(2,1)S(1)}, bf16[4,16,512]{2,1,0:T(8,128)(2,1)S(1)}, u32[]{:S(2)}, u32[]{:S(2)}) collective-permute-start(bf16[4,16,512]{2,1,0:T(8,128)(2,1)S(1)} %pad_maximum_fusion.1), channel_id=1, source_target_pairs={{0,128},{32,160},{64,192},{96,224},{128,0},{160,32},{192,64},{224,... | collective-permute-start | bytes 196616 | tf_op jit(solution)/shard_map/ppermute | solution.py:100
  65.4 16.1 %collective-permute-start.3 = (bf16[24,16,256]{2,1,0:T(8,128)(2,1)S(1)}, bf16[24,16,256]{2,1,0:T(8,128)(2,1)S(1)}, u32[]{:S(2)}, u32[]{:S(2)}) collective-permute-start(bf16[24,16,256]{2,1,0:T(8,128)(2,1)S(1)} %get-tuple-element.36), channel_id=1, source_target_pairs={{0,32},{32,64},{64,96},{96,128},{128,160},{160,192},{192,224},{1,3... | collective-permute-start | bytes 589832 | tf_op jit(solution)/shard_map/ppermute | solution.py:341
  70.2 11.4 %collective-permute-start.4 = (bf16[24,16,256]{2,1,0:T(8,128)(2,1)S(1)}, bf16[24,16,256]{2,1,0:T(8,128)(2,1)S(1)}, u32[]{:S(2)}, u32[]{:S(2)}) collective-permute-start(bf16[24,16,256]{2,1,0:T(8,128)(2,1)S(1)} %get-tuple-element.35), channel_id=1, source_target_pairs={{32,0},{64,32},{96,64},{128,96},{160,128},{192,160},{224,192},{33,... | collective-permute-start | bytes 589832 | tf_op jit(solution)/shard_map/ppermute | solution.py:342

commit v5 on v4

--- a/solution.py
+++ b/solution.py
@@ -18,7 +18,7 @@
 BLOCK = 32
 WIDE_BLOCK = BLOCK + 2 * REACH
 COLS = 160
-UNROLL = 2
+UNROLL = 8
 FIRST = 24
 EARLY = FIRST + 2 * REACH
 LATE = WIDE_BLOCK - EARLY
@@ -190,7 +190,7 @@
         )
         return carry
 
-    lax.fori_loop(0, BLOCK * NB // CHUNK, some_pairs, 0)
+    lax.fori_loop(0, BLOCK * NB // CHUNK, some_pairs, 0, unroll=4)
 
 
 def weights_and_factors(data, choice):
@@ -243,7 +243,7 @@
                 )
         return carry
 
-    lax.fori_loop(0, width, regroup, 0, unroll=2)
+    lax.fori_loop(0, width, regroup, 0, unroll=4)
     if early:
         edge_ref[...] = near[count:]
     else:
@@ -261,7 +261,7 @@
             blend[(place - offset + REACH) * NB + d] = mixed[64 * d : 64 * (d + 1)]
         return carry
 
-    lax.fori_loop(0, count + 2 * REACH, blend_from, 0, unroll=2)
+    lax.fori_loop(0, count + 2 * REACH, blend_from, 0, unroll=7 if early else 6)
 
     def one_atom(atom):
         total = jnp.zeros((64, 256), jnp.float32)

time: 107 us -> 103 us (0.963)
  Pallas kernels: 16.2 us -> 12 us
    pallas_call x2, Pallas kernels: 10.6 us -> 7.02 us  [self_energy_of(): pl.pallas_call(functools.partial(atoms_kernel, begin, end), out_shape=[ou...]
  transfers between devices with their start and end apart: 8 -> 8, of which waited for: 3 -> 3; matrix products, arithmetic and copies ran while one was open for 1% -> 1% of each run, Pallas kernels for 10% -> 7%
where the time goes in v5:
time: 103 us
  starting transfers between devices  33.1 us (32%)
  blocking collectives  30.6 us (30%)
  waiting for transfers between devices  24.5 us (24%)
  Pallas kernels  12 us (12%)
  local copies, waits for them, and re-layouts  1.72 us (2%)
    all_to_all x1, blocking collectives, group_exchange(): lax.all_to_all(blocks, ('x', 'm'), split_axis=0, concat_axis=0, tiled=True)  21.3 us
    ppermute x3, waiting for transfers between devices, atom_data(): held = jnp.concatenate([held, lax.ppermute(held, 'z', pairs)], axis=0)  13.4 us
    ppermute x3, starting transfers between devices, atom_data(): held = jnp.concatenate([held, lax.ppermute(held, 'z', pairs)], axis=0)  13.4 us
    all_to_all x1, waiting for transfers between devices, group_exchange(): lax.all_to_all(blocks, ('x', 'm'), split_axis=0, concat_axis=0, tiled=True)  11.1 us
    all_to_all x1, blocking collectives, group_data(): lax.all_to_all(sorted_pieces(held), 'm', split_axis=0, concat_axis=0, til...  9.32 us
    all_to_all x1, starting transfers between devices, group_exchange(): lax.all_to_all(blocks, ('x', 'm'), split_axis=0, concat_axis=0, tiled=True)  8.72 us
    ppermute x2, starting transfers between devices, exchanged(): below = lax.ppermute(own[NM:, rows], 'z', up)  8.34 us
    pallas_call x2, Pallas kernels, self_energy_of(): pl.pallas_call(functools.partial(atoms_kernel, begin, end), out_shape=[ou...  7.02 us
  transfers between devices with their start and end apart: 8, of which 3 were waited for; matrix products, arithmetic and copies ran while one was open for 1% of the time, Pallas kernels for 7%

profile of v5, /device:TPU:1, one launch (start us, length us, event | category | flops | bytes accessed | tf_op | source)
XLA Modules:
  0.0 102.7 jit_solution(11661205237639859237)
XLA Ops:
  0.0 2.4 %shard_map.64 = bf16[32,72,256]{2,1,0:T(8,128)(2,1)} custom-call(bf16[2,1024,256]{2,1,0:T(8,128)(2,1)} %bitcast.14), custom_call_target="tpu_custom_call" | custom-call | flops 4194304 | bytes 2097152 | tf_op jit(solution)/shard_map/pallas_call | solution.py:66
  2.4 0.0 copy-start.1
  2.4 0.0 copy-start.3
  2.4 0.0 copy-start.4
  2.4 0.0 copy-start.2
  2.4 8.7 %all-to-all-start = ((bf16[32,72,256]{2,1,0:T(8,128)(2,1)}), bf16[32,72,256]{2,1,0:T(8,128)(2,1)S(1)}, u32[]{:S(2)}, u32[]{:S(2)}) async-start(bf16[32,72,256]{2,1,0:T(8,128)(2,1)} %shard_map.64), calls=%async_computation | async-start | bytes 2359296 | tf_op jit(solution)/shard_map/all_to_all | solution.py:30
  11.3 0.1 subtract_select_fusion
  11.3 0.1 broadcast_compare_fusion
  11.4 0.1 select_reduce_fusion
  11.5 0.1 convert_element_type.23
  11.7 0.1 select_reduce_fusion.1
  11.8 0.2 copy.11
  12.0 0.1 convert_element_type.25
  12.1 0.1 tile.9
  12.2 1.7 %collective-permute-start = (bf16[1,16,512]{2,1,0:T(8,128)(2,1)S(1)}, bf16[1,16,512]{2,1,0:T(8,128)(2,1)S(1)}, u32[]{:S(2)}, u32[]{:S(2)}) collective-permute-start(bf16[1,16,512]{2,1,0:T(8,128)(2,1)S(1)} %maximum_bitcast_fusion), channel_id=1, source_target_pairs={{0,32},{32,0},{64,96},{96,64},{128,160},{160,128},{192,224},{224,1... | collective-permute-start | bytes 49160 | tf_op jit(solution)/shard_map/ppermute | solution.py:100
  13.9 1.4 %collective-permute-done = bf16[1,16,512]{2,1,0:T(8,128)(2,1)S(1)} collective-permute-done((bf16[1,16,512]{2,1,0:T(8,128)(2,1)S(1)}, bf16[1,16,512]{2,1,0:T(8,128)(2,1)S(1)}, u32[]{:S(2)}, u32[]{:S(2)}) %collective-permute-start) | collective-permute-done | bytes 16416 | tf_op jit(solution)/shard_map/ppermute | solution.py:100
  15.4 3.1 %collective-permute-start.1 = (bf16[2,16,512]{2,1,0:T(8,128)(2,1)S(1)}, bf16[2,16,512]{2,1,0:T(8,128)(2,1)S(1)}, u32[]{:S(2)}, u32[]{:S(2)}) collective-permute-start(bf16[2,16,512]{2,1,0:T(8,128)(2,1)S(1)} %pad_maximum_fusion.2), channel_id=1, source_target_pairs={{0,64},{32,96},{64,0},{96,32},{128,192},{160,224},{192,128},{224,1... | collective-permute-start | bytes 98312 | tf_op jit(solution)/shard_map/ppermute | solution.py:100
  18.5 11.1 %all-to-all-done.refs_1_ = bf16[32,72,256]{2,1,0:T(8,128)(2,1)S(1)} async-done(((bf16[32,72,256]{2,1,0:T(8,128)(2,1)}), bf16[32,72,256]{2,1,0:T(8,128)(2,1)S(1)}, u32[]{:S(2)}, u32[]{:S(2)}) %all-to-all-start) | async-done | bytes 1179680 | tf_op jit(solution)/shard_map/all_to_all | solution.py:30
  29.5 0.1 fusion
  29.6 3.6 %collective-permute-start.5 = (bf16[24,56,256]{2,1,0:T(8,128)(2,1)S(1)}, bf16[24,56,256]{2,1,0:T(8,128)(2,1)S(1)}, u32[]{:S(2)}, u32[]{:S(2)}) collective-permute-start(bf16[24,56,256]{2,1,0:T(8,128)(2,1)S(1)} %get-tuple-element.34), channel_id=1, source_target_pairs={{0,32},{32,64},{64,96},{96,128},{128,160},{160,192},{192,224},{1,3... | collective-permute-start | bytes 2064392 | tf_op jit(solution)/shard_map/ppermute | solution.py:341
  33.2 1.3 %collective-permute-start.6 = (bf16[24,56,256]{2,1,0:T(8,128)(2,1)S(1)}, bf16[24,56,256]{2,1,0:T(8,128)(2,1)S(1)}, u32[]{:S(2)}, u32[]{:S(2)}) collective-permute-start(bf16[24,56,256]{2,1,0:T(8,128)(2,1)S(1)} %get-tuple-element.33), channel_id=1, source_target_pairs={{32,0},{64,32},{96,64},{128,96},{160,128},{192,160},{224,192},{33,... | collective-permute-start | bytes 2064392 | tf_op jit(solution)/shard_map/ppermute | solution.py:342
  34.5 8.6 %collective-permute-start.2 = (bf16[4,16,512]{2,1,0:T(8,128)(2,1)S(1)}, bf16[4,16,512]{2,1,0:T(8,128)(2,1)S(1)}, u32[]{:S(2)}, u32[]{:S(2)}) collective-permute-start(bf16[4,16,512]{2,1,0:T(8,128)(2,1)S(1)} %pad_maximum_fusion.1), channel_id=1, source_target_pairs={{0,128},{32,160},{64,192},{96,224},{128,0},{160,32},{192,64},{224,... | collective-permute-start | bytes 196616 | tf_op jit(solution)/shard_map/ppermute | solution.py:100
  43.2 0.8 shard_map.65.choice_ref
  44.0 12.0 %collective-permute-done.2 = bf16[4,16,512]{2,1,0:T(8,128)(2,1)S(1)} collective-permute-done((bf16[4,16,512]{2,1,0:T(8,128)(2,1)S(1)}, bf16[4,16,512]{2,1,0:T(8,128)(2,1)S(1)}, u32[]{:S(2)}, u32[]{:S(2)}) %collective-permute-start.2) | collective-permute-done | bytes 65568 | tf_op jit(solution)/shard_map/ppermute | solution.py:100
  56.0 9.3 %all_to_all.15 = bf16[8,16,512]{2,1,0:T(8,128)(2,1)S(1)} all-to-all(bf16[8,16,512]{2,1,0:T(8,128)(2,1)S(1)} %shard_map.66), channel_id=1, replica_groups=mesh['z'=8,'x'=4,'m'=8] {'m'}, dimensions={0} | all-to-all | bytes 262144 | tf_op jit(solution)/shard_map/all_to_all | solution.py:123
  65.4 4.8 %collective-permute-start.3 = (bf16[24,16,256]{2,1,0:T(8,128)(2,1)S(1)}, bf16[24,16,256]{2,1,0:T(8,128)(2,1)S(1)}, u32[]{:S(2)}, u32[]{:S(2)}) collective-permute-start(bf16[24,16,256]{2,1,0:T(8,128)(2,1)S(1)} %get-tuple-element.36), channel_id=1, source_target_pairs={{0,32},{32,64},{64,96},{96,128},{128,160},{160,192},{192,224},{1,3... | collective-permute-start | bytes 589832 | tf_op jit(solution)/shard_map/ppermute | solution.py:341
  70.2 1.3 %collective-permute-start.4 = (bf16[24,16,256]{2,1,0:T(8,128)(2,1)S(1)}, bf16[24,16,256]{2,1,0:T(8,128)(2,1)S(1)}, u32[]{:S(2)}, u32[]{:S(2)}) collective-permute-start(bf16[24,16,256]{2,1,0:T(8,128)(2,1)S(1)} %get-tuple-element.35), channel_id=1, source_target_pairs={{32,0},{64,32},{96,64},{128,96},{160,128},{192,160},{224,192},{33,... | collective-permute-start | bytes 589832 | tf_op jit(solution)/shard_map/ppermute | solution.py:342
  71.5 1.8 %shard_map.67 = (bf16[128,64,256]{2,1,0:T(8,128)(2,1)S(1)}, f32[2048,512]{1,0:T(8,128)S(1)}) custom-call(bf16[128,512]{1,0:T(8,128)(2,1)S(1)} %bitcast.12, bf16[256,2048]{1,0:T(8,128)(2,1)S(1)} %shard_map.65.choice_ref), custom_call_target="tpu_custom_call" | custom-call | flops 1073741824 | bytes 6291456 | tf_op jit(solution)/shard_map/pallas_call | solution.py:198
  73.3 5.1 %shard_map.68 = (bf16[32,64,256]{2,1,0:T(8,128)(2,1)S(1)}, bf16[4,160,256]{2,1,0:T(8,128)(2,1)S(1)}) custom-call(bf16[24,56,256]{2,1,0:T(8,128)(2,1)S(1)} %collective-permute-done.5.refs_0_, bf16[32,72,256]{2,1,0:T(8,128)(2,1)S(1)} %all-to-all-done.refs_1_, bf16[24,56,256]{2,1,0:T(8,128)(2,1)S(1)} %collective-permute-done.6.refs_2_, ...), custom_call_target="tpu_custom_call" | custom-call | flops 1308622848 | bytes 8388608 | tf_op jit(solution)/shard_map/pallas_call | solution.py:315
  78.4 2.0 %shard_map.69 = bf16[32,64,256]{2,1,0:T(8,128)(2,1)S(1)} custom-call(bf16[24,16,256]{2,1,0:T(8,128)(2,1)S(1)} %collective-permute-done.3.refs_0_, bf16[32,72,256]{2,1,0:T(8,128)(2,1)S(1)} %all-to-all-done.refs_1_, bf16[24,16,256]{2,1,0:T(8,128)(2,1)S(1)} %collective-permute-done.4.refs_2_, bf16[128,64,256]{2,1,0:T(8,128)(2,1)S(1)} %get-tuple-element.29.refs_3_, ...), custom_call_target="tpu_custom_call" | custom-call | flops 436207616 | bytes 8388608 | tf_op jit(solution)/shard_map/pallas_call | solution.py:315
  80.3 21.3 %all_to_all.16 = bf16[32,64,256]{2,1,0:T(8,128)(2,1)S(1)} all-to-all(bf16[32,64,256]{2,1,0:T(8,128)(2,1)S(1)} %shard_map.69), channel_id=1, replica_groups=mesh['z'=8,'x'=4,'m'=8] {'x','m'}, dimensions={0} | all-to-all | bytes 2097152 | tf_op jit(solution)/shard_map/all_to_all | solution.py:30
  101.7 1.1 %copy.12 = bf16[2,8,4,32,256]{4,3,2,1,0:T(8,128)(2,1)} copy(bf16[2,8,4,32,256]{4,3,0,1,2:T(8,128)(2,1)S(1)} %bitcast.13) | data formatting | bytes 2097152 | tf_op jit(solution)/shard_map/transpose | solution.py:360
  (21 shorter events, 0.1 us)
Async XLA Ops:
  2.4 8.8 %copy-start.1 = (bf16[4,4,16,16]{3,2,1,0:T(8,128)(2,1)S(1)}, bf16[4,4,16,16]{3,2,1,0:T(8,128)(2,1)}, u32[]{:S(2)}) copy-start(bf16[4,4,16,16]{3,2,1,0:T(8,128)(2,1)} %param.10) | copy-start | bytes 24580
  2.4 8.8 %copy-start.3 = (s32[4,4]{1,0:T(4,128)S(1)}, s32[4,4]{1,0:T(4,128)}, u32[]{:S(2)}) copy-start(s32[4,4]{1,0:T(4,128)} %param.7) | copy-start | bytes 196
  2.4 8.8 %copy-start.4 = (s32[4]{0:T(128)S(1)}, s32[4]{0:T(128)}, u32[]{:S(2)}) copy-start(s32[4]{0:T(128)} %param.8) | copy-start | bytes 52
  2.4 9.2 %copy-start.2 = (f32[4,4,8,4]{2,3,1,0:T(4,128)S(1)}, f32[4,4,8,4]{2,3,1,0:T(4,128)}, u32[]{:S(2)}) copy-start(f32[4,4,8,4]{2,3,1,0:T(4,128)} %param.9) | copy-start | bytes 6148
  2.4 27.1 %all-to-all-start = ((bf16[32,72,256]{2,1,0:T(8,128)(2,1)}), bf16[32,72,256]{2,1,0:T(8,128)(2,1)S(1)}, u32[]{:S(2)}, u32[]{:S(2)}) async-start(bf16[32,72,256]{2,1,0:T(8,128)(2,1)} %shard_map.64), calls=%async_computation | async-start | bytes 2359296 | tf_op jit(solution)/shard_map/all_to_all | solution.py:30
  12.2 3.1 %collective-permute-start = (bf16[1,16,512]{2,1,0:T(8,128)(2,1)S(1)}, bf16[1,16,512]{2,1,0:T(8,128)(2,1)S(1)}, u32[]{:S(2)}, u32[]{:S(2)}) collective-permute-start(bf16[1,16,512]{2,1,0:T(8,128)(2,1)S(1)} %maximum_bitcast_fusion), channel_id=1, source_target_pairs={{0,32},{32,0},{64,96},{96,64},{128,160},{160,128},{192,224},{224,1... | collective-permute-start | bytes 49160 | tf_op jit(solution)/shard_map/ppermute | solution.py:100
  15.4 27.8 %copy-start = (s32[8,8]{1,0:T(8,128)S(1)}, s32[8,8]{1,0:T(8,128)}, u32[]{:S(2)}) copy-start(s32[8,8]{1,0:T(8,128)} %table_ref.1) | copy-start | bytes 772
  15.4 19.1 %collective-permute-start.1 = (bf16[2,16,512]{2,1,0:T(8,128)(2,1)S(1)}, bf16[2,16,512]{2,1,0:T(8,128)(2,1)S(1)}, u32[]{:S(2)}, u32[]{:S(2)}) collective-permute-start(bf16[2,16,512]{2,1,0:T(8,128)(2,1)S(1)} %pad_maximum_fusion.2), channel_id=1, source_target_pairs={{0,64},{32,96},{64,0},{96,32},{128,192},{160,224},{192,128},{224,1... | collective-permute-start | bytes 98312 | tf_op jit(solution)/shard_map/ppermute | solution.py:100
  29.6 43.7 %collective-permute-start.5 = (bf16[24,56,256]{2,1,0:T(8,128)(2,1)S(1)}, bf16[24,56,256]{2,1,0:T(8,128)(2,1)S(1)}, u32[]{:S(2)}, u32[]{:S(2)}) collective-permute-start(bf16[24,56,256]{2,1,0:T(8,128)(2,1)S(1)} %get-tuple-element.34), channel_id=1, source_target_pairs={{0,32},{32,64},{64,96},{96,128},{128,160},{160,192},{192,224},{1,3... | collective-permute-start | bytes 2064392 | tf_op jit(solution)/shard_map/ppermute | solution.py:341
  33.2 40.1 %collective-permute-start.6 = (bf16[24,56,256]{2,1,0:T(8,128)(2,1)S(1)}, bf16[24,56,256]{2,1,0:T(8,128)(2,1)S(1)}, u32[]{:S(2)}, u32[]{:S(2)}) collective-permute-start(bf16[24,56,256]{2,1,0:T(8,128)(2,1)S(1)} %get-tuple-element.33), channel_id=1, source_target_pairs={{32,0},{64,32},{96,64},{128,96},{160,128},{192,160},{224,192},{33,... | collective-permute-start | bytes 2064392 | tf_op jit(solution)/shard_map/ppermute | solution.py:342
  34.5 21.4 %collective-permute-start.2 = (bf16[4,16,512]{2,1,0:T(8,128)(2,1)S(1)}, bf16[4,16,512]{2,1,0:T(8,128)(2,1)S(1)}, u32[]{:S(2)}, u32[]{:S(2)}) collective-permute-start(bf16[4,16,512]{2,1,0:T(8,128)(2,1)S(1)} %pad_maximum_fusion.1), channel_id=1, source_target_pairs={{0,128},{32,160},{64,192},{96,224},{128,0},{160,32},{192,64},{224,... | collective-permute-start | bytes 196616 | tf_op jit(solution)/shard_map/ppermute | solution.py:100
  65.4 13.0 %collective-permute-start.3 = (bf16[24,16,256]{2,1,0:T(8,128)(2,1)S(1)}, bf16[24,16,256]{2,1,0:T(8,128)(2,1)S(1)}, u32[]{:S(2)}, u32[]{:S(2)}) collective-permute-start(bf16[24,16,256]{2,1,0:T(8,128)(2,1)S(1)} %get-tuple-element.36), channel_id=1, source_target_pairs={{0,32},{32,64},{64,96},{96,128},{128,160},{160,192},{192,224},{1,3... | collective-permute-start | bytes 589832 | tf_op jit(solution)/shard_map/ppermute | solution.py:341
  70.2 8.2 %collective-permute-start.4 = (bf16[24,16,256]{2,1,0:T(8,128)(2,1)S(1)}, bf16[24,16,256]{2,1,0:T(8,128)(2,1)S(1)}, u32[]{:S(2)}, u32[]{:S(2)}) collective-permute-start(bf16[24,16,256]{2,1,0:T(8,128)(2,1)S(1)} %get-tuple-element.35), channel_id=1, source_target_pairs={{32,0},{64,32},{96,64},{128,96},{160,128},{192,160},{224,192},{33,... | collective-permute-start | bytes 589832 | tf_op jit(solution)/shard_map/ppermute | solution.py:342
